TPU v7x, 32 devices: a whole 2x2x4 slice. The times are simulated.
32 devices in a mesh: tm: 4 (over x, core), batch: 8 (over z, y).
Axes of the slice: x: 2, y: 2, z: 4, core: 2. Of those that a mesh axis runs over, the one named last changes fastest.
Arguments:
- initial_state: float32 [2048, 256], P('batch'), may hold values from -6 to 6
- increments: float32 [32, 2048, 256], P('tm', 'batch'), may hold values from -1.5 to 1.5
- cotangents: float32 [32, 2048, 256], P('tm', 'batch'), may hold values from -1.5 to 1.5
- drift_inner: bfloat16 [256, 1024], replicated, may hold values from -0.375 to 0.375
- drift_hidden: float32 [1024], replicated, may hold values from -3 to 3
- drift_outer: bfloat16 [1024, 256], replicated, may hold values from -0.1875 to 0.1875
- drift_offset: float32 [256], replicated, may hold values from -3 to 3
- noise_inner: bfloat16 [256, 1024], replicated, may hold values from -0.375 to 0.375
- noise_hidden: float32 [1024], replicated, may hold values from -3 to 3
- noise_outer: bfloat16 [1024, 256], replicated, may hold values from -0.1875 to 0.1875
- noise_offset: float32 [256], replicated, may hold values from -4 to 4
Outputs:
- states: float32 [32, 2048, 256], P('tm', 'batch')
- adjoints: float32 [32, 2048, 256], P('tm', 'batch')
- drift_inner_grad: float32 [256, 1024], replicated
- drift_hidden_grad: float32 [1024], replicated
- drift_outer_grad: float32 [1024, 256], replicated
- drift_offset_grad: float32 [256], replicated
- noise_inner_grad: float32 [256, 1024], replicated
- noise_hidden_grad: float32 [1024], replicated
- noise_outer_grad: float32 [1024, 256], replicated
- noise_offset_grad: float32 [256], replicated
All inputs are finite; a program needn't handle non-finite values.
Results may differ from a plain program's by a relative error of at most 0.0095.
Values sent between devices are 32-bit elements; how exact they have to be, the bound alone decides.
No kernel may reach another device: no remote copies, remote signals or barrier semaphores. Data moves between devices by JAX's collectives and lax.ppermute only.
A program may use at most 128 MiB of HBM per device.

v0:
```python
import math

import jax
import jax.numpy as jnp
from jax import lax
from jax.sharding import PartitionSpec as P

L = 256
H = 1024


delta_time = 0.05


def shifted(block, axis, distance):
    devices = range(lax.axis_size(axis))
    route = [(i - distance, i) for i in devices if i - distance in devices]
    return lax.ppermute(block, axis, route)


def matmul(left, right):
    return jnp.dot(left, right, preferred_element_type=jnp.float32)


def matmul_transposed(left, right):
    return lax.dot_general(
        left, right, (((1,), (1,)), ((), ())), preferred_element_type=jnp.float32
    )


def matmul_rows(left, right):
    return lax.dot_general(
        left, right, (((0,), (0,)), ((), ())), preferred_element_type=jnp.float32
    )


def advance(state, noise, params):
    (
        drift_inner,
        drift_hidden,
        drift_outer,
        drift_offset,
        noise_inner,
        noise_hidden,
        noise_outer,
        noise_offset,
    ) = params
    state_low = state.astype(jnp.bfloat16)
    hidden_drift = jnp.tanh(matmul(state_low, drift_inner) + drift_hidden).astype(jnp.bfloat16)
    hidden_noise = jnp.tanh(matmul(state_low, noise_inner) + noise_hidden).astype(jnp.bfloat16)
    drift = matmul(hidden_drift, drift_outer) + drift_offset
    spread = jax.nn.sigmoid(matmul(hidden_noise, noise_outer) + noise_offset)
    return (
        state + delta_time * drift + spread * noise,
        (state_low, hidden_drift, hidden_noise, spread),
    )


def retreat(adjoint_next, state, noise, params):
    (
        drift_inner,
        drift_hidden,
        drift_outer,
        drift_offset,
        noise_inner,
        noise_hidden,
        noise_outer,
        noise_offset,
    ) = params
    unused, saved = advance(state, noise, params)
    state_low, hidden_drift, hidden_noise, spread = saved
    drift_grad = delta_time * adjoint_next
    noise_grad = adjoint_next * noise * spread * (1.0 - spread)
    drift_low = drift_grad.astype(jnp.bfloat16)
    noise_low = noise_grad.astype(jnp.bfloat16)
    back_drift = matmul_transposed(drift_low, drift_outer) * (
        1.0 - jnp.square(hidden_drift.astype(jnp.float32))
    )
    back_noise = matmul_transposed(noise_low, noise_outer) * (
        1.0 - jnp.square(hidden_noise.astype(jnp.float32))
    )
    back_drift_low = back_drift.astype(jnp.bfloat16)
    back_noise_low = back_noise.astype(jnp.bfloat16)
    adjoint = (
        adjoint_next
        + matmul_transposed(back_drift_low, drift_inner)
        + matmul_transposed(back_noise_low, noise_inner)
    )
    grads = (
        matmul_rows(state_low, back_drift_low),
        jnp.sum(back_drift, 0),
        matmul_rows(hidden_drift, drift_low),
        jnp.sum(drift_grad, 0),
        matmul_rows(state_low, back_noise_low),
        jnp.sum(back_noise, 0),
        matmul_rows(hidden_noise, noise_low),
        jnp.sum(noise_grad, 0),
    )
    return (adjoint, grads)


def squares(grads):
    total = jnp.sum(jnp.square(grads[0]))
    for entry in grads[1:]:
        total = total + jnp.sum(jnp.square(entry))
    return total


def clip_factor(total):
    limit = 0.5 * math.sqrt(4 * L * H + 2 * H + 2 * L)
    return jnp.minimum(1.0, limit / jnp.sqrt(total))


def shards(
    initial_state,
    increments,
    cotangents,
    drift_inner,
    drift_hidden,
    drift_outer,
    drift_offset,
    noise_inner,
    noise_hidden,
    noise_outer,
    noise_offset,
):
    params = (
        drift_inner,
        drift_hidden,
        drift_outer,
        drift_offset,
        noise_inner,
        noise_hidden,
        noise_outer,
        noise_offset,
    )
    segments = lax.axis_size("tm")
    segment = lax.axis_index("tm")
    steps_here, rows, width = increments.shape
    blocks = 2
    block_rows = rows // blocks
    rounds = blocks + segments - 1

    def run_forward(operand):
        start_state, block, states, entries = operand
        offset = block * block_rows
        noise_block = lax.dynamic_slice_in_dim(increments, offset, block_rows, 1)
        state = start_state
        produced = []
        for index in range(steps_here):
            state, unused = advance(state, noise_block[index], params)
            produced.append(state)
        states = lax.dynamic_update_slice_in_dim(states, jnp.stack(produced), offset, 1)
        entries = lax.dynamic_update_slice_in_dim(entries, start_state, offset, 0)
        return (state, states, entries)

    def skip_forward(operand):
        start_state, block, states, entries = operand
        return (jnp.zeros_like(start_state), states, entries)

    def forward_round(turn, carry):
        incoming, states, entries = carry
        block = turn - segment
        valid = (block >= 0) & (block < blocks)
        clamped = jnp.clip(block, 0, blocks - 1)
        own = lax.dynamic_slice_in_dim(initial_state, clamped * block_rows, block_rows, 0)
        start_state = jnp.where(segment == 0, own, incoming)
        outgoing, states, entries = lax.cond(
            valid, run_forward, skip_forward, (start_state, clamped, states, entries)
        )
        incoming = shifted(outgoing, "tm", 1)
        return (incoming, states, entries)

    start = (
        jnp.zeros((block_rows, width), jnp.float32),
        jnp.zeros_like(increments),
        jnp.zeros_like(initial_state),
    )
    unused, states, entries = lax.fori_loop(0, rounds, forward_round, start)

    def run_backward(operand):
        adjoint, block, adjoints, totals = operand
        offset = block * block_rows
        noise_block = lax.dynamic_slice_in_dim(increments, offset, block_rows, 1)
        cotangent_block = lax.dynamic_slice_in_dim(cotangents, offset, block_rows, 1)
        state_block = lax.dynamic_slice_in_dim(states, offset, block_rows, 1)
        entry = lax.dynamic_slice_in_dim(entries, offset, block_rows, 0)
        column = [None] * steps_here
        for index in reversed(range(steps_here)):
            before = entry if index == 0 else state_block[index - 1]
            adjoint, grads = retreat(
                adjoint + cotangent_block[index], before, noise_block[index], params
            )
            totals = tuple((a + b for a, b in zip(totals, grads)))
            column[index] = adjoint
        adjoints = lax.dynamic_update_slice_in_dim(adjoints, jnp.stack(column), offset, 1)
        return (adjoint, adjoints, totals)

    def skip_backward(operand):
        adjoint, block, adjoints, totals = operand
        return (jnp.zeros_like(adjoint), adjoints, totals)

    def backward_round(turn, carry):
        incoming, adjoints, totals = carry
        block = turn - (segments - 1 - segment)
        valid = (block >= 0) & (block < blocks)
        clamped = jnp.clip(block, 0, blocks - 1)
        outgoing, adjoints, totals = lax.cond(
            valid, run_backward, skip_backward, (incoming, clamped, adjoints, totals)
        )
        incoming = shifted(outgoing, "tm", -1)
        return (incoming, adjoints, totals)

    blank = tuple((jnp.zeros(p.shape, jnp.float32) for p in params))
    start = (jnp.zeros((block_rows, width), jnp.float32), jnp.zeros_like(increments), blank)
    unused, adjoints, totals = lax.fori_loop(0, rounds, backward_round, start)
    summed = lax.psum(
        (totals[0], totals[1], totals[2], totals[3], totals[4], totals[5], totals[6], totals[7]),
        ("tm", "batch"),
    )
    factor = clip_factor(squares(summed))
    result = tuple((entry * factor for entry in summed))
    return (
        states,
        adjoints,
        result[0],
        result[1],
        result[2],
        result[3],
        result[4],
        result[5],
        result[6],
        result[7],
    )


def solution(mesh):
    placed = (
        P("batch", None),
        P("tm", "batch", None),
        P("tm", "batch", None),
        P(),
        P(),
        P(),
        P(),
        P(),
        P(),
        P(),
        P(),
    )
    return jax.shard_map(
        shards,
        mesh=mesh,
        in_specs=placed,
        out_specs=(
            P("tm", "batch", None),
            P("tm", "batch", None),
            P(),
            P(),
            P(),
            P(),
            P(),
            P(),
            P(),
            P(),
        ),
        check_vma=False,
    )
```

profile of v0, /device:TPU:0, one launch (start us, length us, event | category | flops | bytes accessed | tf_op | source)
XLA Modules:
  0.0 786.6 jit_solution(2424366928954173790)
XLA Ops:
  9.5 93.3 %while.51 = (s32[]{:T(128)}, f32[128,256]{1,0:T(8,128)S(1)}, f32[8,256,256]{2,1,0:T(8,128)}, bf16[256,256]{1,0:T(8,128)(2,1)}, s32[]{:T(128)}, /*index=5*/pred[]...) while((s32[]{:T(128)}, f32[128,256]{1,0:T(8,128)S(1)}, ...), condition=%wide.region_3.4_spmd, body=%wide.region_0.3_spmd.sunk | while | flops 2154594304 | bytes 28394616 | solution.py:179
  9.5 17.4 %conditional.4 = (f32[128,256]{1,0:T(8,128)}, f32[8,256,256]{2,1,0:T(8,128)}, bf16[256,256]{1,0:T(8,128)(2,1)}) conditional(s32[]{:T(128)} %convert_element_type.851, (f32[8,256,256]{2,1,0:T(8,128)}, bf16[256,256]{1,0:T(8,128)(2,1)}) %tuple.170, (pred[]{:T(512)}, s32[]{:T(128)}, f32[256,256]{1,0:T(8,128)}, f32[128,256]{1,0:T(8,128)S(1)}, ...), branch_computations={%region_1.1_spmd, %region_2.2_spmd} | conditional | flops 2154594304 | bytes 27869942 | solution.py:168
  29.4 17.4 %conditional.4 = (f32[128,256]{1,0:T(8,128)}, f32[8,256,256]{2,1,0:T(8,128)}, bf16[256,256]{1,0:T(8,128)(2,1)}) conditional(s32[]{:T(128)} %convert_element_type.851, (f32[8,256,256]{2,1,0:T(8,128)}, bf16[256,256]{1,0:T(8,128)(2,1)}) %tuple.170, (pred[]{:T(512)}, s32[]{:T(128)}, f32[256,256]{1,0:T(8,128)}, f32[128,256]{1,0:T(8,128)S(1)}, ...), branch_computations={%region_1.1_spmd, %region_2.2_spmd} | conditional | flops 2154594304 | bytes 27869942 | solution.py:168
  46.8 2.3 collective-permute-start
  50.9 19.7 %collective-permute-start = (f32[128,256]{1,0:T(8,128)}, f32[128,256]{1,0:T(8,128)S(1)}, u32[]{:S(2)}, u32[]{:S(2)}) collective-permute-start(f32[128,256]{1,0:T(8,128)} %get-tuple-element.1600), channel_id=1, source_target_pairs={{0,8},{8,16},{16,24},{1,9},{9,17},{17,25},{2,10},{10,18},{18,26},{... | collective-permute-start | bytes 393224 | tf_op jit(solution)/shard_map/while/body/eval_jaxpr/ppermute | solution.py:18
  72.5 5.3 collective-permute-start
  79.6 22.0 %collective-permute-start = (f32[128,256]{1,0:T(8,128)}, f32[128,256]{1,0:T(8,128)S(1)}, u32[]{:S(2)}, u32[]{:S(2)}) collective-permute-start(f32[128,256]{1,0:T(8,128)} %get-tuple-element.1600), channel_id=1, source_target_pairs={{0,8},{8,16},{16,24},{1,9},{9,17},{17,25},{2,10},{10,18},{18,26},{... | collective-permute-start | bytes 393224 | tf_op jit(solution)/shard_map/while/body/eval_jaxpr/ppermute | solution.py:18
  102.8 2.7 convert.30
  112.6 504.2 %while.52 = (s32[]{:T(128)}, f32[128,256]{1,0:T(8,128)S(1)}, f32[8,256,256]{2,1,0:T(8,128)}, f32[256,1024]{1,0:T(8,128)S(1)}, f32[1024]{0:T(1024)}, /*index=5*/f...) while((s32[]{:T(128)}, f32[128,256]{1,0:T(8,128)S(1)}, ...), condition=%wide.region_39.40_spmd, body=%wide.region_4.39_spmd.sunk | while | flops 5935726592 | bytes 240598432 | solution.py:216
  114.6 5.1 collective-permute-done.1
  121.7 16.1 %collective-permute-done.1 = f32[128,256]{1,0:T(8,128)S(1)} collective-permute-done((f32[128,256]{1,0:T(8,128)}, f32[128,256]{1,0:T(8,128)S(1)}, u32[]{:S(2)}, u32[]{:S(2)}) %collective-permute-start.1) | collective-permute-done | bytes 131104 | tf_op jit(solution)/shard_map/while/body/eval_jaxpr/ppermute | solution.py:18
  139.7 280.0 %collective-permute-done.1 = f32[128,256]{1,0:T(8,128)S(1)} collective-permute-done((f32[128,256]{1,0:T(8,128)}, f32[128,256]{1,0:T(8,128)S(1)}, u32[]{:S(2)}, u32[]{:S(2)}) %collective-permute-start.1) | collective-permute-done | bytes 131104 | tf_op jit(solution)/shard_map/while/body/eval_jaxpr/ppermute | solution.py:18
  419.8 92.9 %conditional.5 = (f32[128,256]{1,0:T(8,128)S(1)}, f32[8,256,256]{2,1,0:T(8,128)}, f32[256,1024]{1,0:T(8,128)S(1)}, f32[1024]{0:T(1024)}, f32[1024,256]{1,0:T(8,1...) conditional(s32[]{:T(128)} %convert_element_type.852, ...), branch_computations={%region_5.5_spmd, %region_6.38_spmd} | conditional | flops 5935726592 | bytes 239549264 | solution.py:208
  428.0 2.5 multiply_reduce_fusion.6
  438.0 2.5 multiply_reduce_fusion.5
  448.2 2.6 multiply_reduce_fusion.4
  459.3 2.6 multiply_reduce_fusion.3
  470.4 2.6 multiply_reduce_fusion.2
  494.3 2.2 convolution_add_fusion.24
  514.6 5.2 collective-permute-done.1
  519.8 92.9 %conditional.5 = (f32[128,256]{1,0:T(8,128)S(1)}, f32[8,256,256]{2,1,0:T(8,128)}, f32[256,1024]{1,0:T(8,128)S(1)}, f32[1024]{0:T(1024)}, f32[1024,256]{1,0:T(8,1...) conditional(s32[]{:T(128)} %convert_element_type.852, ...), branch_computations={%region_5.5_spmd, %region_6.38_spmd} | conditional | flops 5935726592 | bytes 239549264 | solution.py:208
  528.1 2.5 multiply_reduce_fusion.6
  538.1 2.5 multiply_reduce_fusion.5
  548.3 2.6 multiply_reduce_fusion.4
  559.4 2.6 multiply_reduce_fusion.3
  570.5 2.6 multiply_reduce_fusion.2
  594.4 2.2 convolution_add_fusion.24
  614.7 2.1 collective-permute-done.1
  617.8 42.0 %all-reduce = (f32[1024]{0:T(1024)S(1)}, f32[256]{0:T(256)S(1)}, f32[1024]{0:T(1024)S(1)}, f32[256]{0:T(256)S(1)}) all-reduce(f32[1024]{0:T(1024)} %get-tuple-element.1132, f32[256]{0:T(256)} %get-tuple-element.1134, f32[1024]{0:T(1024)} %get-tuple-element.1136, ...), channel_id=1, replica_groups=mesh['tm'=4,'batch'=8] {'tm','batch'}, use_global_device_ids=true, to_apply=%region_42.43 | all-reduce | flops 2560 | bytes 20480 | tf_op jit(solution)/shard_map/psum | solution.py:217
  661.7 101.5 %all-reduce.4.cloned.1.call-done = (f32[256,1024]{1,0:T(8,128)}, f32[1024,256]{1,0:T(8,128)}, f32[256,1024]{1,0:T(8,128)}, f32[1024,256]{1,0:T(8,128)}) async-done(((f32[256,1024]{1,0:T(8,128)}, f32[1024,256]{1,0:T(8,128)}, f32[256,1024]{1,0:T(8,128)}, f32[1024,256]{1,0:T(8,128)}), (f32[256,1024]{1,0:T(8,128)}, f32[1024,256]{1,0:T(8,128)}, f32[256,1024]{1,0:T(8,128)}, ...) | async-done | bytes 4194320 | tf_op jit(solution)/shard_map/psum | solution.py:217
  763.2 2.6 multiply_reduce_fusion.8
  772.5 2.4 broadcast_multiply_fusion
  (621 shorter events, 227.5 us)
Async XLA Ops:
  7.2 756.0 %all-reduce.4.cloned.1.call-start = ((), (), s32[]{:S(2)}) async-start(), calls=%async_computation | async-start | bytes 8388608 | tf_op jit(solution)/shard_map/psum | solution.py:217
  27.0 2.5 collective-permute-start
  46.8 3.4 collective-permute-start
  50.9 20.9 %collective-permute-start = (f32[128,256]{1,0:T(8,128)}, f32[128,256]{1,0:T(8,128)S(1)}, u32[]{:S(2)}, u32[]{:S(2)}) collective-permute-start(f32[128,256]{1,0:T(8,128)} %get-tuple-element.1600), channel_id=1, source_target_pairs={{0,8},{8,16},{16,24},{1,9},{9,17},{17,25},{2,10},{10,18},{18,26},{... | collective-permute-start | bytes 393224 | tf_op jit(solution)/shard_map/while/body/eval_jaxpr/ppermute | solution.py:18
  72.5 6.5 collective-permute-start
  79.6 23.2 %collective-permute-start = (f32[128,256]{1,0:T(8,128)}, f32[128,256]{1,0:T(8,128)S(1)}, u32[]{:S(2)}, u32[]{:S(2)}) collective-permute-start(f32[128,256]{1,0:T(8,128)} %get-tuple-element.1600), channel_id=1, source_target_pairs={{0,8},{8,16},{16,24},{1,9},{9,17},{17,25},{2,10},{10,18},{18,26},{... | collective-permute-start | bytes 393224 | tf_op jit(solution)/shard_map/while/body/eval_jaxpr/ppermute | solution.py:18
  113.3 6.3 collective-permute-start.1
  120.4 17.4 %collective-permute-start.1 = (f32[128,256]{1,0:T(8,128)}, f32[128,256]{1,0:T(8,128)S(1)}, u32[]{:S(2)}, u32[]{:S(2)}) collective-permute-start(f32[128,256]{1,0:T(8,128)} %copy-done.65), channel_id=1, source_target_pairs={{8,0},{16,8},{24,16},{9,1},{17,9},{25,17},{10,2},{18,10},{26,18},{... | collective-permute-start | bytes 393224 | tf_op jit(solution)/shard_map/while/body/eval_jaxpr/ppermute | solution.py:18
  138.4 281.3 %collective-permute-start.1 = (f32[128,256]{1,0:T(8,128)}, f32[128,256]{1,0:T(8,128)S(1)}, u32[]{:S(2)}, u32[]{:S(2)}) collective-permute-start(f32[128,256]{1,0:T(8,128)} %copy-done.65), channel_id=1, source_target_pairs={{8,0},{16,8},{24,16},{9,1},{17,9},{25,17},{10,2},{18,10},{26,18},{... | collective-permute-start | bytes 393224 | tf_op jit(solution)/shard_map/while/body/eval_jaxpr/ppermute | solution.py:18
  428.0 4.6 copy-start.51
  428.0 4.6 copy-start.60
  430.5 6.4 copy-start.36
  440.5 6.0 copy-start.38
  448.2 4.6 copy-start.6
  450.9 6.8 copy-start.40
  459.3 4.7 copy-start.7
  462.0 6.8 copy-start.42
  470.4 4.6 copy-start.8
  473.1 6.8 copy-start.44
  513.3 6.5 collective-permute-start.1
  528.0 4.6 copy-start.51
  528.1 4.6 copy-start.60
  530.6 6.4 copy-start.36
  540.6 6.0 copy-start.38
  548.3 4.6 copy-start.6
  550.9 6.8 copy-start.40
  559.4 4.7 copy-start.7
  562.0 6.8 copy-start.42
  570.5 4.6 copy-start.8
  573.1 6.8 copy-start.44
  613.4 3.4 collective-permute-start.1
  772.5 4.6 copy-start.62
  (153 other events, 295.0 us)
Sparse Core Ops, SparseCore 0:
  618.0 145.2 all-reduce.3
where the time goes:
time: 789 us; the launch traced here: 787 us
  waiting for transfers between devices  416 us (53%)
  matrix products  175 us (22%)
  starting transfers between devices  57 us (7%)
  local copies, waits for them, and re-layouts  46.9 us (6%)
  blocking collectives  42 us (5%)
  other arithmetic  27.2 us (3%)
  between operations  19.4 us (2%)
    ppermute x10, waiting for transfers between devices, shifted(): return lax.ppermute(block, axis, route)  314 us
    psum x1, waiting for transfers between devices, shards(): lax.psum((totals[0], totals[1], totals[2], totals[3], totals[4], totals[5...  102 us
    dot_general x64, matrix products, matmul_transposed(): lax.dot_general(left, right, (((1,), (1,)), ((), ())), preferred_element_...  69.6 us
    dot_general x80, matrix products, matmul(): return jnp.dot(left, right, preferred_element_type=jnp.float32)  66.4 us
    ppermute x10, starting transfers between devices, shifted(): return lax.ppermute(block, axis, route)  57 us
    psum x1, blocking collectives, shards(): lax.psum((totals[0], totals[1], totals[2], totals[3], totals[4], totals[5...  42 us
    dot_general x64, matrix products, matmul_rows(): lax.dot_general(left, right, (((0,), (0,)), ((), ())), preferred_element_...  39.4 us
    cond x328, local copies, waits for them, and re-layouts  26.8 us
  transfers between devices with their start and end apart: 11, of which 11 were waited for; matrix products, arithmetic and copies ran while one was open for 0% of the time, Pallas kernels for 0%

commit v1 on v0

v1 whole, which is shorter than its diff:
```python
import functools
import math

import jax
import jax.numpy as jnp
from jax import lax
from jax.experimental import pallas as pl
from jax.experimental.pallas import tpu as pltpu
from jax.sharding import PartitionSpec as P

delta_time = 0.05
TILE = 256
LANES = 128
COLORS = 3
PARAMS = pltpu.CompilerParams(vmem_limit_bytes=60 * 1024 * 1024)
ANY = pl.BlockSpec(memory_space=pl.ANY)
VMEM = pl.BlockSpec(memory_space=pltpu.VMEM)
SMEM = pl.BlockSpec(memory_space=pltpu.SMEM)


def dot(left, right):
    return jnp.dot(left, right, preferred_element_type=jnp.float32)


def dot_rows(left, right):
    return lax.dot_general(
        left, right, (((0,), (0,)), ((), ())), preferred_element_type=jnp.float32
    )


def step_copies(own, received, core, half, rows, steps, buffer, sems, k):
    local = lax.rem(k, steps)
    from_own = pltpu.make_async_copy(
        own.at[local, pl.ds(pl.multiple_of(core * rows, 8), rows), :], buffer.at[k], sems.at[k]
    )
    from_mate = pltpu.make_async_copy(received.at[local], buffer.at[k], sems.at[k])
    return from_own, from_mate


def forward_kernel(
    full,
    steps,
    rows,
    info,
    initial,
    incoming,
    own_noise,
    mate_noise,
    drift_inner,
    drift_hidden,
    drift_outer,
    drift_offset,
    noise_inner,
    noise_hidden,
    noise_outer,
    noise_offset,
    *rest,
):
    if full:
        final, states, states_send, q_out, u_out, v_out, a_out = rest[:7]
        noise_buf, in_sems, out_sem, z_buf, q_buf, u_buf, v_buf, a_buf = rest[7:]
    else:
        final, noise_buf, in_sems = rest
    window = 2 * steps
    core = info[0]
    first = info[1]
    hidden = drift_inner.shape[1]

    def start(k, carry):
        mine = k // steps == core
        from_own, from_mate = step_copies(
            own_noise, mate_noise, core, None, rows, steps, noise_buf, in_sems, k
        )

        @pl.when(mine)
        def _():
            from_own.start()

        @pl.when(jnp.logical_not(mine))
        def _():
            from_mate.start()

        return carry

    lax.fori_loop(0, window, start, 0)
    begin = jnp.where(first == 1, initial[pl.ds(pl.multiple_of(core * rows, 8), rows), :], incoming[...])

    def state_copies(k):
        local = lax.rem(k, steps)
        keep = pltpu.make_async_copy(
            z_buf.at[k],
            states.at[local, pl.ds(pl.multiple_of(core * rows, 8), rows), :],
            out_sem,
        )
        send = pltpu.make_async_copy(z_buf.at[k], states_send.at[local], out_sem)
        return keep, send

    def saved_copies(k):
        return [
            pltpu.make_async_copy(buf.at[k], out.at[k], out_sem)
            for buf, out in ((q_buf, q_out), (u_buf, u_out), (v_buf, v_out), (a_buf, a_out))
        ]

    def body(k, state):
        pltpu.make_async_copy(mate_noise.at[0], noise_buf.at[k], in_sems.at[k]).wait()
        q = state.astype(jnp.bfloat16)
        if full:
            q_buf[k] = q
        drift = drift_offset[...]
        spread = noise_offset[...]
        for j in range(hidden // TILE):
            cols = slice(j * TILE, (j + 1) * TILE)
            u = jnp.tanh(dot(q, drift_inner[:, cols]) + drift_hidden[:, cols]).astype(jnp.bfloat16)
            v = jnp.tanh(dot(q, noise_inner[:, cols]) + noise_hidden[:, cols]).astype(jnp.bfloat16)
            if full:
                u_buf[k, :, cols] = u
                v_buf[k, :, cols] = v
            drift = drift + dot(u, drift_outer[cols, :])
            spread = spread + dot(v, noise_outer[cols, :])
        s = 0.5 * jnp.tanh(0.5 * spread) + 0.5
        noise = noise_buf[k]
        following = state + delta_time * drift + s * noise
        if full:
            a_buf[k] = noise * s * (1.0 - s)
            z_buf[k] = following
            mine = k // steps == core
            keep, send = state_copies(k)

            @pl.when(mine)
            def _():
                keep.start()

            @pl.when(jnp.logical_not(mine))
            def _():
                send.start()

            for copy in saved_copies(k):
                copy.start()
        return following

    final[...] = lax.fori_loop(0, window, body, begin)
    if full:

        def finish(k, carry):
            state_copies(k)[1].wait()
            for copy in saved_copies(k):
                copy.wait()
            return carry

        lax.fori_loop(0, window, finish, 0)


def backward_kernel(
    full,
    steps,
    rows,
    blocks,
    block_rows,
    info,
    incoming,
    own_cotangent,
    mate_cotangent,
    q_in,
    u_in,
    v_in,
    a_in,
    drift_inner_t,
    drift_outer_t,
    noise_inner_t,
    noise_outer_t,
    *rest,
):
    if full:
        final, adjoints, adjoints_send, keep_out, send_out = rest[:5]
        (c_buf, u_buf, v_buf, a_buf, in_sems, q_sem, out_sem, q_buf) = rest[5:13]
        (e_buf, pb_buf, rb_buf, fb_buf, gb_buf, p_sum, r_sum, f_sum, g_sum, packed) = rest[13:]
    else:
        final, c_buf, u_buf, v_buf, a_buf, in_sems = rest
    window = 2 * steps
    core = info[0]
    last = info[2]
    width, hidden = drift_outer_t.shape

    def saved_copies(k):
        return [
            pltpu.make_async_copy(src.at[k], buf.at[k], in_sems.at[k])
            for src, buf in ((u_in, u_buf), (v_in, v_buf), (a_in, a_buf))
        ]

    def start(n, carry):
        k = window - 1 - n
        mine = k // steps == core
        from_own, from_mate = step_copies(
            own_cotangent, mate_cotangent, core, None, rows, steps, c_buf, in_sems, k
        )

        @pl.when(mine)
        def _():
            from_own.start()

        @pl.when(jnp.logical_not(mine))
        def _():
            from_mate.start()

        for copy in saved_copies(k):
            copy.start()
        return carry

    lax.fori_loop(0, window, start, 0)
    if full:
        pltpu.make_async_copy(q_in, q_buf, q_sem).start()
        for ref in (p_sum, r_sum, f_sum, g_sum):
            ref[...] = jnp.zeros_like(ref)
    begin = jnp.where(last == 1, jnp.zeros_like(incoming), incoming[...])

    def adjoint_copies(k):
        local = lax.rem(k, steps)
        keep = pltpu.make_async_copy(
            e_buf.at[k],
            adjoints.at[local, pl.ds(pl.multiple_of(core * rows, 8), rows), :],
            out_sem,
        )
        send = pltpu.make_async_copy(e_buf.at[k], adjoints_send.at[local], out_sem)
        return keep, send

    def partial(x):
        return jnp.sum(x.reshape(rows // 8, 8, x.shape[1]), 0)

    def body(n, adjoint):
        k = window - 1 - n
        pltpu.make_async_copy(mate_cotangent.at[0], c_buf.at[k], in_sems.at[k]).wait()
        for copy in saved_copies(k):
            copy.wait()
        w = adjoint + c_buf[k]
        f = delta_time * w
        g = w * a_buf[k]
        fb = f.astype(jnp.bfloat16)
        gb = g.astype(jnp.bfloat16)
        if full:
            fb_buf[k] = fb
            gb_buf[k] = gb
            f_sum[...] += partial(f)
            g_sum[...] += partial(g)
        result = w
        for j in range(hidden // TILE):
            cols = slice(j * TILE, (j + 1) * TILE)
            u = u_buf[k, :, cols].astype(jnp.float32)
            v = v_buf[k, :, cols].astype(jnp.float32)
            p = dot(fb, drift_outer_t[:, cols]) * (1.0 - u * u)
            r = dot(gb, noise_outer_t[:, cols]) * (1.0 - v * v)
            pb = p.astype(jnp.bfloat16)
            rb = r.astype(jnp.bfloat16)
            if full:
                p_sum[:, cols] += partial(p)
                r_sum[:, cols] += partial(r)
                pb_buf[k, :, cols] = pb
                rb_buf[k, :, cols] = rb
            result = result + dot(pb, drift_inner_t[cols, :])
            result = result + dot(rb, noise_inner_t[cols, :])
        if full:
            e_buf[k] = result
            mine = k // steps == core
            keep, send = adjoint_copies(k)

            @pl.when(mine)
            def _():
                keep.start()

            @pl.when(jnp.logical_not(mine))
            def _():
                send.start()

        return result

    final[...] = lax.fori_loop(0, window, body, begin)
    if not full:
        return
    pltpu.make_async_copy(q_in, q_buf, q_sem).wait()
    total = window * rows
    q = q_buf[...].reshape(total, width)
    per_matrix = width * hidden // LANES
    nets = (
        (pb_buf, fb_buf, u_buf, p_sum, f_sum),
        (rb_buf, gb_buf, v_buf, r_sum, g_sum),
    )
    for net, (back_buf, low_buf, hid_buf, hidden_sum, offset_sum) in enumerate(nets):
        low = low_buf[...].reshape(total, width)
        for j in range(hidden // TILE):
            cols = slice(j * TILE, (j + 1) * TILE)
            inner = dot_rows(q, back_buf[:, :, cols].reshape(total, TILE))
            outer = dot_rows(low, hid_buf[:, :, cols].reshape(total, TILE))
            for i in range(TILE // LANES):
                row = (j * (TILE // LANES) + i) * width
                lanes = slice(i * LANES, (i + 1) * LANES)
                packed[net, row : row + width, :] = inner[:, lanes]
                packed[net, per_matrix + row : per_matrix + row + width, :] = outer[:, lanes]
        base = 2 * per_matrix
        hidden_total = jnp.sum(hidden_sum[...], 0, keepdims=True)
        offset_total = jnp.sum(offset_sum[...], 0, keepdims=True)
        packed[net, base:, :] = jnp.zeros((packed.shape[1] - base, LANES), jnp.float32)
        for i in range(hidden // LANES):
            packed[net, base + i : base + i + 1, :] = hidden_total[:, i * LANES : (i + 1) * LANES]
        base += hidden // LANES
        for i in range(width // LANES):
            packed[net, base + i : base + i + 1, :] = offset_total[:, i * LANES : (i + 1) * LANES]

    def grad_copies(out, net):
        copies = []
        for color in range(COLORS):
            me = info[3 + color]
            for s in range(blocks):
                source = (color * blocks + s) * block_rows
                place = color * blocks + ((s ^ (blocks - 1)) ^ me)
                copies.append(
                    pltpu.make_async_copy(
                        packed.at[net, pl.ds(source, block_rows), :],
                        out.at[pl.ds(pl.multiple_of(place * block_rows, 8), block_rows), :],
                        out_sem,
                    )
                )
        return copies

    for copy in grad_copies(send_out, 1 - core) + grad_copies(keep_out, core):
        copy.start()

    def finish(k, carry):
        adjoint_copies(k)[1].wait()
        return carry

    lax.fori_loop(0, window, finish, 0)
    for copy in grad_copies(send_out, 1 - core) + grad_copies(keep_out, core):
        copy.wait()


def finish_kernel(blocks, block_rows, width, hidden, limit, info, *rest):
    pieces = rest[: 4 * COLORS]
    outs = rest[4 * COLORS : 4 * COLORS + 8]
    packed, sem = rest[4 * COLORS + 8 :]
    core = info[0]
    half = blocks // 2
    copies = []
    for color in range(COLORS):
        me = info[3 + color]
        for side in range(2):
            net = core if side == 0 else 1 - core
            for top in range(2):
                piece = pieces[color * 4 + side * 2 + top]
                for p in range(half):
                    s = (top * half + half - 1 - p) ^ me
                    place = (color * blocks + s) * block_rows
                    copies.append(
                        pltpu.make_async_copy(
                            piece.at[pl.ds(p * block_rows, block_rows), :],
                            packed.at[net, pl.ds(pl.multiple_of(place, 8), block_rows), :],
                            sem,
                        )
                    )
    for copy in copies:
        copy.start()
    for copy in copies:
        copy.wait()
    chunk = block_rows * blocks * COLORS // 8
    acc = jnp.zeros((8, LANES), jnp.float32)
    for net in range(2):
        whole = packed[net]
        acc = acc + jnp.sum(jnp.square(whole).reshape(chunk, 8, LANES), 0)
    total = jnp.sum(jnp.sum(acc, 1, keepdims=True), 0, keepdims=True)
    factor = jnp.minimum(1.0, limit / jnp.sqrt(total))
    per_matrix = width * hidden // LANES
    for net in range(2):
        inner, hidden_out, outer, offset_out = outs[net * 4 : net * 4 + 4]
        for j in range(hidden // LANES):
            lanes = slice(j * LANES, (j + 1) * LANES)
            inner[:, lanes] = packed[net, j * width : (j + 1) * width, :] * factor
            row = per_matrix + j * width
            outer[lanes, :] = (packed[net, row : row + width, :] * factor).T
        base = 2 * per_matrix
        for j in range(hidden // LANES):
            hidden_out[:, j * LANES : (j + 1) * LANES] = packed[net, base + j : base + j + 1, :] * factor
        base += hidden // LANES
        for j in range(width // LANES):
            offset_out[:, j * LANES : (j + 1) * LANES] = packed[net, base + j : base + j + 1, :] * factor


def flipped(block, axis, bit):
    return lax.ppermute(block, axis, [(i, i ^ bit) for i in range(lax.axis_size(axis))])


def moved(block, distance):
    count = lax.axis_size("tm")
    return lax.ppermute(
        block, "tm", [(i, i + distance) for i in range(count) if 0 <= i + distance < count]
    )


def bits_of(size):
    return [1 << i for i in range(size.bit_length() - 1)]


def shards(
    initial_state,
    increments,
    cotangents,
    drift_inner,
    drift_hidden,
    drift_outer,
    drift_offset,
    noise_inner,
    noise_hidden,
    noise_outer,
    noise_offset,
):
    f32, bf16 = jnp.float32, jnp.bfloat16
    segments = lax.axis_size("tm")
    segment = lax.axis_index("tm")
    group = lax.axis_index("batch")
    core = segment % 2
    stages = segments // 2
    stage = segment // 2
    steps, local_rows, width = increments.shape
    hidden = drift_inner.shape[1]
    rows = local_rows // 2
    window = 2 * steps

    dims = [("tm", bit) for bit in bits_of(segments)[1:]]
    dims += [("batch", bit) for bit in bits_of(lax.axis_size("batch"))]
    turn = min(COLORS, len(dims))
    orders = [dims[i % turn : turn] + dims[: i % turn] + dims[turn:] for i in range(COLORS)]
    blocks = 1 << len(dims)
    used = (2 * width * hidden + hidden + width) // LANES
    block_rows = 8 * (-(-used // (8 * blocks * COLORS)))
    color_rows = blocks * block_rows
    packed_rows = COLORS * color_rows

    def position(order):
        place = jnp.int32(0)
        for axis, bit in order:
            index = segment if axis == "tm" else group
            place = 2 * place + (index // bit) % 2
        return place

    info = jnp.stack(
        [core, (stage == 0).astype(jnp.int32), (stage == stages - 1).astype(jnp.int32)]
        + [position(order) for order in orders]
    ).astype(jnp.int32)

    def other_half(array):
        return lax.dynamic_slice_in_dim(array, (1 - core) * rows, rows, 1)

    mate_noise = flipped(other_half(increments), "tm", 1)
    mate_cotangent = flipped(other_half(cotangents), "tm", 1)
    weights = (
        drift_inner,
        drift_hidden.reshape(1, hidden),
        drift_outer,
        drift_offset.reshape(1, width),
        noise_inner,
        noise_hidden.reshape(1, hidden),
        noise_outer,
        noise_offset.reshape(1, width),
    )
    turned = (drift_inner.T, drift_outer.T, noise_inner.T, noise_outer.T)

    def sds(shape, dtype=f32):
        return jax.ShapeDtypeStruct(shape, dtype)

    def forward(incoming, full):
        out_shape = [sds((rows, width))]
        out_specs = [VMEM]
        scratch = [
            pltpu.VMEM((window, rows, width), f32),
            pltpu.SemaphoreType.DMA((window,)),
        ]
        if full:
            out_shape += [
                sds((steps, local_rows, width)),
                sds((steps, rows, width)),
                sds((window, rows, width), bf16),
                sds((window, rows, hidden), bf16),
                sds((window, rows, hidden), bf16),
                sds((window, rows, width)),
            ]
            out_specs += [ANY] * 6
            scratch += [
                pltpu.SemaphoreType.DMA,
                pltpu.VMEM((window, rows, width), f32),
                pltpu.VMEM((window, rows, width), bf16),
                pltpu.VMEM((window, rows, hidden), bf16),
                pltpu.VMEM((window, rows, hidden), bf16),
                pltpu.VMEM((window, rows, width), f32),
            ]
        return pl.pallas_call(
            functools.partial(forward_kernel, full, steps, rows),
            out_shape=out_shape,
            in_specs=[SMEM, VMEM, VMEM, ANY, ANY] + [VMEM] * 8,
            out_specs=out_specs,
            scratch_shapes=scratch,
            compiler_params=PARAMS,
            name="forward_full" if full else "forward_light",
        )(info, initial_state, incoming, increments, mate_noise, *weights)

    incoming = jnp.zeros((rows, width), f32)
    for turn_index in range(stages - 1):
        incoming = moved(forward(incoming, False)[0], 2)
    unused, states, states_send, q, u, v, a = forward(incoming, True)
    states_mate = flipped(states_send, "tm", 1)

    def backward(incoming, full):
        out_shape = [sds((rows, width))]
        out_specs = [VMEM]
        scratch = [
            pltpu.VMEM((window, rows, width), f32),
            pltpu.VMEM((window, rows, hidden), bf16),
            pltpu.VMEM((window, rows, hidden), bf16),
            pltpu.VMEM((window, rows, width), f32),
            pltpu.SemaphoreType.DMA((window,)),
        ]
        if full:
            out_shape += [
                sds((steps, local_rows, width)),
                sds((steps, rows, width)),
                sds((packed_rows, LANES)),
                sds((packed_rows, LANES)),
            ]
            out_specs += [ANY] * 4
            scratch += [
                pltpu.SemaphoreType.DMA,
                pltpu.SemaphoreType.DMA,
                pltpu.VMEM((window, rows, width), bf16),
                pltpu.VMEM((window, rows, width), f32),
                pltpu.VMEM((window, rows, hidden), bf16),
                pltpu.VMEM((window, rows, hidden), bf16),
                pltpu.VMEM((window, rows, width), bf16),
                pltpu.VMEM((window, rows, width), bf16),
                pltpu.VMEM((8, hidden), f32),
                pltpu.VMEM((8, hidden), f32),
                pltpu.VMEM((8, width), f32),
                pltpu.VMEM((8, width), f32),
                pltpu.VMEM((2, packed_rows, LANES), f32),
            ]
        return pl.pallas_call(
            functools.partial(backward_kernel, full, steps, rows, blocks, block_rows),
            out_shape=out_shape,
            in_specs=[SMEM, VMEM] + [ANY] * 6 + [VMEM] * 4,
            out_specs=out_specs,
            scratch_shapes=scratch,
            compiler_params=PARAMS,
            name="backward_full" if full else "backward_light",
        )(info, incoming, cotangents, mate_cotangent, q, u, v, a, *turned)

    incoming = jnp.zeros((rows, width), f32)
    for turn_index in range(stages - 1):
        incoming = moved(backward(incoming, False)[0], -2)
    unused, adjoints, adjoints_send, keep, send = backward(incoming, True)
    mate_grads = flipped(send, "tm", 1)
    adjoints_mate = flipped(adjoints_send, "tm", 1)

    parts = [[keep, mate_grads] for order in orders]
    starts = [[i * color_rows] * 2 for i in range(COLORS)]
    size = color_rows

    def gathered(i, begin, count):
        total = None
        for part, start in zip(parts[i], starts[i]):
            piece = part[start + begin : start + begin + count]
            total = piece if total is None else total + piece
        return total

    for phase in range(len(dims)):
        size //= 2
        arrived = [flipped(gathered(i, 0, size), *orders[i][phase]) for i in range(COLORS)]
        for i in range(COLORS):
            starts[i] = [start + size for start in starts[i]] + [0]
            parts[i].append(arrived[i])
    current = [gathered(i, 0, size) for i in range(COLORS)]
    for phase in reversed(range(1, len(dims))):
        arrived = [flipped(current[i], *orders[i][phase]) for i in range(COLORS)]
        current = [jnp.concatenate([arrived[i], current[i]], 0) for i in range(COLORS)]
    low_mate = [flipped(current[i], "tm", 1) for i in range(COLORS)]
    top = [flipped(current[i], *orders[i][0]) for i in range(COLORS)]
    top_mate = [flipped(top[i], "tm", 1) for i in range(COLORS)]
    pieces = []
    for i in range(COLORS):
        pieces += [current[i], top[i], low_mate[i], top_mate[i]]

    limit = 0.5 * math.sqrt(4 * width * hidden + 2 * hidden + 2 * width)
    shapes = [(width, hidden), (1, hidden), (hidden, width), (1, width)] * 2
    grads = pl.pallas_call(
        functools.partial(finish_kernel, blocks, block_rows, width, hidden, limit),
        out_shape=[sds(shape) for shape in shapes],
        in_specs=[SMEM] + [ANY] * len(pieces),
        out_specs=[VMEM] * 8,
        scratch_shapes=[
            pltpu.VMEM((2, packed_rows, LANES), f32),
            pltpu.SemaphoreType.DMA,
        ],
        compiler_params=PARAMS,
        name="finish",
    )(info, *pieces)
    grads = [g.reshape(-1) if g.shape[0] == 1 else g for g in grads]
    far = (1 - core) * rows
    states = lax.dynamic_update_slice_in_dim(states, states_mate, far, 1)
    adjoints = lax.dynamic_update_slice_in_dim(adjoints, adjoints_mate, far, 1)
    return (states, adjoints, *grads)


def solution(mesh):
    placed = (P("batch", None), P("tm", "batch", None), P("tm", "batch", None)) + (P(),) * 8
    return jax.shard_map(
        shards,
        mesh=mesh,
        in_specs=placed,
        out_specs=(P("tm", "batch", None), P("tm", "batch", None)) + (P(),) * 8,
        check_vma=False,
    )
```

time: 789 us -> 175 us (0.22)
  waiting for transfers between devices: 416 us -> 45.7 us
  matrix products: 175 us -> 0 us
  Pallas kernels: 0 us -> 73.8 us
  blocking collectives: 42 us -> 0 us
  local copies, waits for them, and re-layouts: 46.9 us -> 13.9 us
  other arithmetic: 27.2 us -> 1.8 us
  starting transfers between devices: 57 us -> 38.4 us
  between operations: 19.4 us -> 1.21 us
    ppermute x10 -> x37, waiting for transfers between devices: 314 us -> 45.7 us  [the longest x35 39.9 us: flipped(): lax.ppermute(block, axis, [(i, i ^ bit) for i in range(lax.axis_size(axis...]
    dot_general x208 -> x0, matrix products: 175 us -> none  [the longest x64 69.6 us: matmul_transposed(): lax.dot_general(left, right, (((1,), (1,)), ((), ())), preferred_element_...]
    psum x1 -> x0, waiting for transfers between devices: 102 us -> none  [shards(): lax.psum((totals[0], totals[1], totals[2], totals[3], totals[4], totals[5...]
    pallas_call x0 -> x5, Pallas kernels: none -> 73.8 us  [the longest x2 36.8 us: forward(): pl.pallas_call(functools.partial(forward_kernel, full, steps, rows), out_...]
    psum x1 -> x0, blocking collectives: 42 us -> none  [shards(): lax.psum((totals[0], totals[1], totals[2], totals[3], totals[4], totals[5...]
    cond x328 -> x0, local copies, waits for them, and re-layouts: 26.8 us -> none
    ppermute x10 -> x37, starting transfers between devices: 57 us -> 38.4 us  [the longest x35 32 us: flipped(): lax.ppermute(block, axis, [(i, i ^ bit) for i in range(lax.axis_size(axis...]
    another operation x22 -> x2, local copies, waits for them, and re-layouts: 12.8 us -> 1.27 us
  transfers between devices with their start and end apart: 11 -> 37, of which waited for: 11 -> 20; matrix products, arithmetic and copies ran while one was open for 0% -> 4% of each run, Pallas kernels for 0% -> 21%
where the time goes in v1:
time: 175 us
  Pallas kernels  73.8 us (42%)
  waiting for transfers between devices  45.7 us (26%)
  starting transfers between devices  38.4 us (22%)
  local copies, waits for them, and re-layouts  13.9 us (8%)
  other arithmetic  1.8 us (1%)
    ppermute x35, waiting for transfers between devices, flipped(): lax.ppermute(block, axis, [(i, i ^ bit) for i in range(lax.axis_size(axis...  39.9 us
    pallas_call x2, Pallas kernels, forward(): pl.pallas_call(functools.partial(forward_kernel, full, steps, rows), out_...  36.8 us
    ppermute x35, starting transfers between devices, flipped(): lax.ppermute(block, axis, [(i, i ^ bit) for i in range(lax.axis_size(axis...  32 us
    pallas_call x2, Pallas kernels, backward(): pl.pallas_call(functools.partial(backward_kernel, full, steps, rows, bloc...  31.2 us
    unnamed x56, local copies, waits for them, and re-layouts  8.92 us
    ppermute x2, starting transfers between devices, moved(): lax.ppermute(block, 'tm', [(i, i + distance) for i in range(count) if 0 <...  6.36 us
    ppermute x2, waiting for transfers between devices, moved(): lax.ppermute(block, 'tm', [(i, i + distance) for i in range(count) if 0 <...  5.87 us
    pallas_call x1, Pallas kernels, shards(): pl.pallas_call(functools.partial(finish_kernel, blocks, block_rows, width...  5.79 us
  transfers between devices with their start and end apart: 37, of which 20 were waited for; matrix products, arithmetic and copies ran while one was open for 4% of the time, Pallas kernels for 21%

profile of v1, /device:TPU:0, one launch (start us, length us, event | category | flops | bytes accessed | tf_op | source)
XLA Modules:
  0.0 174.7 jit_solution(9777235366670553710)
XLA Ops:
  0.7 2.4 %constant_dynamic-slice_fusion.1 = f32[8,128,256]{2,1,0:T(8,128)} fusion(f32[8,256,256]{2,1,0:T(8,128)} %own_noise.3, s32[]{:T(128)S(6)} %select_n.73), kind=kLoop, calls=%fused_computation.57 | loop fusion | bytes 2097156 | tf_op jit(solution)/shard_map/dynamic_slice | solution.py:448
  6.9 17.9 %forward_light.1 = f32[128,256]{1,0:T(8,128)} custom-call(s32[6]{0:T(128)} %stack.35.info, f32[256,256]{1,0:T(8,128)} %initial.3, f32[128,256]{1,0:T(8,128)} %broadcast_1_incoming.2.incoming, f32[8,256,256]{2,1,0:T(8,128)} %own_noise.3, f32[8,128,256]{2,1,0:T(8,128)} %collective-permute-done.mate_noise, bf16[256,1024]{1,0:T(8,128)(2,1)} %drift_inner.3, ...), custom_call_target="tpu_custom_call" | custom-call | tf_op jit(solution)/shard_map/forward_light/pallas_call | solution.py:492
  24.8 4.9 %collective-permute-start.1 = (f32[128,256]{1,0:T(8,128)}, f32[128,256]{1,0:T(8,128)S(1)}, u32[]{:S(2)}, u32[]{:S(2)}) collective-permute-start(f32[128,256]{1,0:T(8,128)} %forward_light.1), channel_id=1, source_target_pairs={{0,16},{8,24},{1,17},{9,25},{2,18},{10,26},{3,19},{11,27},{4,20},{... | collective-permute-start | bytes 393224 | tf_op jit(solution)/shard_map/ppermute | solution.py:391
  34.5 18.9 %forward_full.1 = (f32[128,256]{1,0:T(8,128)}, f32[8,256,256]{2,1,0:T(8,128)}, f32[8,128,256]{2,1,0:T(8,128)}, bf16[16,128,256]{2,1,0:T(8,128)(2,1)}, bf16[16,12...) custom-call(s32[6]{0:T(128)} %stack.35.info, f32[256,256]{1,0:T(8,128)} %initial.3, ...), custom_call_target="tpu_custom_call" | custom-call | tf_op jit(solution)/shard_map/forward_full/pallas_call | solution.py:492
  54.4 12.3 %backward_light.1 = f32[128,256]{1,0:T(8,128)} custom-call(s32[6]{0:T(128)} %stack.35.info, f32[128,256]{1,0:T(8,128)} %broadcast_1_incoming.2.incoming, f32[8,256,256]{2,1,0:T(8,128)} %own_cotangent.3, f32[8,128,256]{2,1,0:T(8,128)} %copy-done.5, bf16[16,128,256]{2,1,0:T(8,128)(2,1)} %get-tuple-element.30.q_in, ...), custom_call_target="tpu_custom_call" | custom-call | tf_op jit(solution)/shard_map/backward_light/pallas_call | solution.py:541
  66.6 1.5 collective-permute-start.4
  68.1 5.9 %collective-permute-done.4.incoming = f32[128,256]{1,0:T(8,128)S(1)} collective-permute-done((f32[128,256]{1,0:T(8,128)}, f32[128,256]{1,0:T(8,128)S(1)}, u32[]{:S(2)}, u32[]{:S(2)}) %collective-permute-start.4) | collective-permute-done | bytes 131104 | tf_op jit(solution)/shard_map/ppermute | solution.py:391
  74.6 18.9 %backward_full.1 = (f32[128,256]{1,0:T(8,128)}, f32[8,256,256]{2,1,0:T(8,128)}, f32[8,128,256]{2,1,0:T(8,128)}, f32[4224,128]{1,0:T(8,128)}, f32[4224,128]{1,0:T(8,128)}) custom-call(s32[6]{0:T(128)} %stack.35.info, f32[128,256]{1,0:T(8,128)} %copy-done.18, f32[8,256,256]{2,1,0:T(8,128)} %own_cotangent.3, f32[8,128,256]{2,1,0:T(8,128)} %copy-done.5, ...), custom_call_target="tpu_custom_call" | custom-call | tf_op jit(solution)/shard_map/backward_full/pallas_call | solution.py:541
  93.6 4.5 %collective-permute-done.6 = f32[4224,128]{1,0:T(8,128)S(1)} collective-permute-done((f32[4224,128]{1,0:T(8,128)}, f32[4224,128]{1,0:T(8,128)S(1)}, u32[]{:S(2)}, u32[]{:S(2)}) %collective-permute-start.6) | collective-permute-done | bytes 2162720 | tf_op jit(solution)/shard_map/ppermute | solution.py:386
  98.1 1.3 slice_add_fusion
  99.4 1.6 collective-permute-start.27
  101.0 1.5 collective-permute-start.17
  102.6 7.4 %collective-permute-done.27 = f32[704,128]{1,0:T(8,128)S(1)} collective-permute-done((f32[704,128]{1,0:T(8,128)S(1)}, f32[704,128]{1,0:T(8,128)S(1)}, u32[]{:S(2)}, u32[]{:S(2)}) %collective-permute-start.27) | collective-permute-done | bytes 360480 | tf_op jit(solution)/shard_map/ppermute | solution.py:386
  113.9 4.2 %collective-permute-done.28 = f32[352,128]{1,0:T(8,128)S(1)} collective-permute-done((f32[352,128]{1,0:T(8,128)S(1)}, f32[352,128]{1,0:T(8,128)S(1)}, u32[]{:S(2)}, u32[]{:S(2)}) %collective-permute-start.28) | collective-permute-done | bytes 180256 | tf_op jit(solution)/shard_map/ppermute | solution.py:386
  119.6 1.7 collective-permute-start.19
  121.3 1.6 collective-permute-start.9
  123.6 2.7 %collective-permute-start.30 = (f32[88,128]{1,0:T(8,128)S(1)}, f32[88,128]{1,0:T(8,128)S(1)}, u32[]{:S(2)}, u32[]{:S(2)}) collective-permute-start(f32[88,128]{1,0:T(8,128)S(1)} %slice_add_fusion.18), channel_id=1, source_target_pairs={{0,4},{1,5},{2,6},{3,7},{4,0},{5,1},{6,2},{7,3},{8,12},{9,13},{10,... | collective-permute-start | bytes 135176 | tf_op jit(solution)/shard_map/ppermute | solution.py:386
  126.2 2.3 %collective-permute-done.30 = f32[88,128]{1,0:T(8,128)S(1)} collective-permute-done((f32[88,128]{1,0:T(8,128)S(1)}, f32[88,128]{1,0:T(8,128)S(1)}, u32[]{:S(2)}, u32[]{:S(2)}) %collective-permute-start.30) | collective-permute-done | bytes 45088 | tf_op jit(solution)/shard_map/ppermute | solution.py:386
  128.6 3.1 %collective-permute-start.20 = (f32[88,128]{1,0:T(8,128)S(1)}, f32[88,128]{1,0:T(8,128)S(1)}, u32[]{:S(2)}, u32[]{:S(2)}) collective-permute-start(f32[88,128]{1,0:T(8,128)S(1)} %get-tuple-element.47), channel_id=1, source_target_pairs={{0,4},{1,5},{2,6},{3,7},{4,0},{5,1},{6,2},{7,3},{8,12},{9,13},{10,... | collective-permute-start | bytes 135176 | tf_op jit(solution)/shard_map/ppermute | solution.py:386
  132.4 2.8 %collective-permute-start.31 = (f32[88,128]{1,0:T(8,128)S(1)}, f32[88,128]{1,0:T(8,128)S(1)}, u32[]{:S(2)}, u32[]{:S(2)}) collective-permute-start(f32[88,128]{1,0:T(8,128)S(1)} %get-tuple-element.46), channel_id=1, source_target_pairs={{0,4},{1,5},{2,6},{3,7},{4,0},{5,1},{6,2},{7,3},{8,12},{9,13},{10,... | collective-permute-start | bytes 135176 | tf_op jit(solution)/shard_map/ppermute | solution.py:386
  135.2 1.9 %collective-permute-done.10 = f32[88,128]{1,0:T(8,128)S(1)} collective-permute-done((f32[88,128]{1,0:T(8,128)S(1)}, f32[88,128]{1,0:T(8,128)S(1)}, u32[]{:S(2)}, u32[]{:S(2)}) %collective-permute-start.10) | collective-permute-done | bytes 45088 | tf_op jit(solution)/shard_map/ppermute | solution.py:386
  137.3 2.8 %collective-permute-start.21 = (f32[88,128]{1,0:T(8,128)S(1)}, f32[88,128]{1,0:T(8,128)S(1)}, u32[]{:S(2)}, u32[]{:S(2)}) collective-permute-start(f32[88,128]{1,0:T(8,128)S(1)} %get-tuple-element.58), channel_id=1, source_target_pairs={{0,4},{1,5},{2,6},{3,7},{4,0},{5,1},{6,2},{7,3},{8,12},{9,13},{10,... | collective-permute-start | bytes 135176 | tf_op jit(solution)/shard_map/ppermute | solution.py:386
  142.2 2.4 %collective-permute-start.12 = (f32[176,128]{1,0:T(8,128)S(1)}, f32[176,128]{1,0:T(8,128)S(1)}, u32[]{:S(2)}, u32[]{:S(2)}) collective-permute-start(f32[176,128]{1,0:T(8,128)S(1)} %pad_maximum_fusion.6), channel_id=1, source_target_pairs={{0,2},{1,3},{2,0},{3,1},{4,6},{5,7},{6,4},{7,5},{8,10},{9,11},{10,... | collective-permute-start | bytes 270344 | tf_op jit(solution)/shard_map/ppermute | solution.py:386
  144.6 2.0 %collective-permute-start.22 = (f32[176,128]{1,0:T(8,128)S(1)}, f32[176,128]{1,0:T(8,128)S(1)}, u32[]{:S(2)}, u32[]{:S(2)}) collective-permute-start(f32[176,128]{1,0:T(8,128)S(1)} %pad_maximum_fusion.7), channel_id=1, source_target_pairs={{0,16},{8,24},{16,0},{24,8},{1,17},{9,25},{17,1},{25,9},{2,18},{10... | collective-permute-start | bytes 270344 | tf_op jit(solution)/shard_map/ppermute | solution.py:386
  149.3 1.3 collective-permute-start.23
  150.6 1.6 collective-permute-done.33
  152.9 2.9 %collective-permute-done.23 = f32[352,128]{1,0:T(8,128)S(1)} collective-permute-done((f32[352,128]{1,0:T(8,128)S(1)}, f32[352,128]{1,0:T(8,128)S(1)}, u32[]{:S(2)}, u32[]{:S(2)}) %collective-permute-start.23) | collective-permute-done | bytes 180256 | tf_op jit(solution)/shard_map/ppermute | solution.py:386
  155.7 1.4 collective-permute-start.14
  157.8 1.9 %collective-permute-done.34.rest_9_ = f32[704,128]{1,0:T(8,128)S(1)} collective-permute-done((f32[704,128]{1,0:T(8,128)S(1)}, f32[704,128]{1,0:T(8,128)S(1)}, u32[]{:S(2)}, u32[]{:S(2)}) %collective-permute-start.34) | collective-permute-done | bytes 360480 | tf_op jit(solution)/shard_map/ppermute | solution.py:386
  160.3 4.1 %collective-permute-done.14.rest_1_ = f32[704,128]{1,0:T(8,128)S(1)} collective-permute-done((f32[704,128]{1,0:T(8,128)S(1)}, f32[704,128]{1,0:T(8,128)S(1)}, u32[]{:S(2)}, u32[]{:S(2)}) %collective-permute-start.14) | collective-permute-done | bytes 360480 | tf_op jit(solution)/shard_map/ppermute | solution.py:386
  164.3 1.6 collective-permute-done.24.rest_5_
  168.8 5.8 %finish.1 = (f32[256,1024]{1,0:T(8,128)}, f32[1,1024]{1,0:T(1,128)}, f32[1024,256]{1,0:T(8,128)}, f32[1,256]{1,0:T(1,128)}, f32[256,1024]{1,0:T(8,128)}, /*index...) custom-call(s32[6]{0:T(128)} %stack.35.info, f32[704,128]{1,0:T(8,128)} %copy-done.8, f32[704,128]{1,0:T(8,128)} %copy-done.12, ...), custom_call_target="tpu_custom_call" | custom-call | tf_op jit(solution)/shard_map/finish/pallas_call | solution.py:588
  (124 shorter events, 26.4 us)
Async XLA Ops:
  4.7 48.7 %collective-permute-start.3 = (f32[8,128,256]{2,1,0:T(8,128)}, f32[8,128,256]{2,1,0:T(8,128)S(1)}, u32[]{:S(2)}, u32[]{:S(2)}) collective-permute-start(f32[8,128,256]{2,1,0:T(8,128)} %constant_dynamic-slice_fusion), channel_id=1, source_target_pairs={{0,8},{8,0},{16,24},{24,16},{1,9},{9,1},{17,25},{25,17},{2,10},{10... | collective-permute-start | bytes 3145736 | tf_op jit(solution)/shard_map/ppermute | solution.py:386
  24.8 9.0 %collective-permute-start.1 = (f32[128,256]{1,0:T(8,128)}, f32[128,256]{1,0:T(8,128)S(1)}, u32[]{:S(2)}, u32[]{:S(2)}) collective-permute-start(f32[128,256]{1,0:T(8,128)} %forward_light.1), channel_id=1, source_target_pairs={{0,16},{8,24},{1,17},{9,25},{2,18},{10,26},{3,19},{11,27},{4,20},{... | collective-permute-start | bytes 393224 | tf_op jit(solution)/shard_map/ppermute | solution.py:391
  66.6 7.3 %collective-permute-start.4 = (f32[128,256]{1,0:T(8,128)}, f32[128,256]{1,0:T(8,128)S(1)}, u32[]{:S(2)}, u32[]{:S(2)}) collective-permute-start(f32[128,256]{1,0:T(8,128)} %backward_light.1), channel_id=1, source_target_pairs={{16,0},{24,8},{17,1},{25,9},{18,2},{26,10},{19,3},{27,11},{20,4},{... | collective-permute-start | bytes 393224 | tf_op jit(solution)/shard_map/ppermute | solution.py:391
  99.4 10.5 %collective-permute-start.27 = (f32[704,128]{1,0:T(8,128)S(1)}, f32[704,128]{1,0:T(8,128)S(1)}, u32[]{:S(2)}, u32[]{:S(2)}) collective-permute-start(f32[704,128]{1,0:T(8,128)S(1)} %get-tuple-element.55), channel_id=1, source_target_pairs={{0,2},{1,3},{2,0},{3,1},{4,6},{5,7},{6,4},{7,5},{8,10},{9,11},{10,... | collective-permute-start | bytes 1081352 | tf_op jit(solution)/shard_map/ppermute | solution.py:386
  101.0 10.2 %collective-permute-start.17 = (f32[704,128]{1,0:T(8,128)S(1)}, f32[704,128]{1,0:T(8,128)S(1)}, u32[]{:S(2)}, u32[]{:S(2)}) collective-permute-start(f32[704,128]{1,0:T(8,128)S(1)} %get-tuple-element.56), channel_id=1, source_target_pairs={{0,1},{1,0},{2,3},{3,2},{4,5},{5,4},{6,7},{7,6},{8,9},{9,8},{10,11... | collective-permute-start | bytes 1081352 | tf_op jit(solution)/shard_map/ppermute | solution.py:386
  102.6 9.9 %collective-permute-start.7 = (f32[704,128]{1,0:T(8,128)S(1)}, f32[704,128]{1,0:T(8,128)S(1)}, u32[]{:S(2)}, u32[]{:S(2)}) collective-permute-start(f32[704,128]{1,0:T(8,128)S(1)} %get-tuple-element.57), channel_id=1, source_target_pairs={{0,16},{8,24},{16,0},{24,8},{1,17},{9,25},{17,1},{25,9},{2,18},{10... | collective-permute-start | bytes 1081352 | tf_op jit(solution)/shard_map/ppermute | solution.py:386
  112.6 5.6 %collective-permute-start.28 = (f32[352,128]{1,0:T(8,128)S(1)}, f32[352,128]{1,0:T(8,128)S(1)}, u32[]{:S(2)}, u32[]{:S(2)}) collective-permute-start(f32[352,128]{1,0:T(8,128)S(1)} %get-tuple-element.52), channel_id=1, source_target_pairs={{0,16},{8,24},{16,0},{24,8},{1,17},{9,25},{17,1},{25,9},{2,18},{10... | collective-permute-start | bytes 540680 | tf_op jit(solution)/shard_map/ppermute | solution.py:386
  112.9 5.5 %collective-permute-start.18 = (f32[352,128]{1,0:T(8,128)S(1)}, f32[352,128]{1,0:T(8,128)S(1)}, u32[]{:S(2)}, u32[]{:S(2)}) collective-permute-start(f32[352,128]{1,0:T(8,128)S(1)} %get-tuple-element.53), channel_id=1, source_target_pairs={{0,2},{1,3},{2,0},{3,1},{4,6},{5,7},{6,4},{7,5},{8,10},{9,11},{10,... | collective-permute-start | bytes 540680 | tf_op jit(solution)/shard_map/ppermute | solution.py:386
  113.4 5.5 %collective-permute-start.8 = (f32[352,128]{1,0:T(8,128)S(1)}, f32[352,128]{1,0:T(8,128)S(1)}, u32[]{:S(2)}, u32[]{:S(2)}) collective-permute-start(f32[352,128]{1,0:T(8,128)S(1)} %get-tuple-element.54), channel_id=1, source_target_pairs={{0,1},{1,0},{2,3},{3,2},{4,5},{5,4},{6,7},{7,6},{8,9},{9,8},{10,11... | collective-permute-start | bytes 540680 | tf_op jit(solution)/shard_map/ppermute | solution.py:386
  119.6 6.7 %collective-permute-start.19 = (f32[176,128]{1,0:T(8,128)S(1)}, f32[176,128]{1,0:T(8,128)S(1)}, u32[]{:S(2)}, u32[]{:S(2)}) collective-permute-start(f32[176,128]{1,0:T(8,128)S(1)} %get-tuple-element.50), channel_id=1, source_target_pairs={{0,16},{8,24},{16,0},{24,8},{1,17},{9,25},{17,1},{25,9},{2,18},{10... | collective-permute-start | bytes 270344 | tf_op jit(solution)/shard_map/ppermute | solution.py:386
  121.3 4.9 %collective-permute-start.9 = (f32[176,128]{1,0:T(8,128)S(1)}, f32[176,128]{1,0:T(8,128)S(1)}, u32[]{:S(2)}, u32[]{:S(2)}) collective-permute-start(f32[176,128]{1,0:T(8,128)S(1)} %get-tuple-element.51), channel_id=1, source_target_pairs={{0,2},{1,3},{2,0},{3,1},{4,6},{5,7},{6,4},{7,5},{8,10},{9,11},{10,... | collective-permute-start | bytes 270344 | tf_op jit(solution)/shard_map/ppermute | solution.py:386
  123.6 5.0 %collective-permute-start.30 = (f32[88,128]{1,0:T(8,128)S(1)}, f32[88,128]{1,0:T(8,128)S(1)}, u32[]{:S(2)}, u32[]{:S(2)}) collective-permute-start(f32[88,128]{1,0:T(8,128)S(1)} %slice_add_fusion.18), channel_id=1, source_target_pairs={{0,4},{1,5},{2,6},{3,7},{4,0},{5,1},{6,2},{7,3},{8,12},{9,13},{10,... | collective-permute-start | bytes 135176 | tf_op jit(solution)/shard_map/ppermute | solution.py:386
  128.6 6.6 %collective-permute-start.20 = (f32[88,128]{1,0:T(8,128)S(1)}, f32[88,128]{1,0:T(8,128)S(1)}, u32[]{:S(2)}, u32[]{:S(2)}) collective-permute-start(f32[88,128]{1,0:T(8,128)S(1)} %get-tuple-element.47), channel_id=1, source_target_pairs={{0,4},{1,5},{2,6},{3,7},{4,0},{5,1},{6,2},{7,3},{8,12},{9,13},{10,... | collective-permute-start | bytes 135176 | tf_op jit(solution)/shard_map/ppermute | solution.py:386
  131.8 5.3 %collective-permute-start.10 = (f32[88,128]{1,0:T(8,128)S(1)}, f32[88,128]{1,0:T(8,128)S(1)}, u32[]{:S(2)}, u32[]{:S(2)}) collective-permute-start(f32[88,128]{1,0:T(8,128)S(1)} %get-tuple-element.48), channel_id=1, source_target_pairs={{0,4},{1,5},{2,6},{3,7},{4,0},{5,1},{6,2},{7,3},{8,12},{9,13},{10,... | collective-permute-start | bytes 135176 | tf_op jit(solution)/shard_map/ppermute | solution.py:386
  131.9 25.3 %collective-permute-start.2 = (f32[8,128,256]{2,1,0:T(8,128)S(1)}, f32[8,128,256]{2,1,0:T(8,128)S(1)}, u32[]{:S(2)}, u32[]{:S(2)}) collective-permute-start(f32[8,128,256]{2,1,0:T(8,128)S(1)} %copy-done.24), channel_id=1, source_target_pairs={{0,8},{8,0},{16,24},{24,16},{1,9},{9,1},{17,25},{25,17},{2,10},{10... | collective-permute-start | bytes 3145736 | tf_op jit(solution)/shard_map/ppermute | solution.py:386
  131.9 26.0 %collective-permute-start.5 = (f32[8,128,256]{2,1,0:T(8,128)S(1)}, f32[8,128,256]{2,1,0:T(8,128)S(1)}, u32[]{:S(2)}, u32[]{:S(2)}) collective-permute-start(f32[8,128,256]{2,1,0:T(8,128)S(1)} %copy-done.25), channel_id=1, source_target_pairs={{0,8},{8,0},{16,24},{24,16},{1,9},{9,1},{17,25},{25,17},{2,10},{10... | collective-permute-start | bytes 3145736 | tf_op jit(solution)/shard_map/ppermute | solution.py:386
  132.4 7.8 %collective-permute-start.31 = (f32[88,128]{1,0:T(8,128)S(1)}, f32[88,128]{1,0:T(8,128)S(1)}, u32[]{:S(2)}, u32[]{:S(2)}) collective-permute-start(f32[88,128]{1,0:T(8,128)S(1)} %get-tuple-element.46), channel_id=1, source_target_pairs={{0,4},{1,5},{2,6},{3,7},{4,0},{5,1},{6,2},{7,3},{8,12},{9,13},{10,... | collective-permute-start | bytes 135176 | tf_op jit(solution)/shard_map/ppermute | solution.py:386
  137.2 5.0 %collective-permute-start.11 = (f32[88,128]{1,0:T(8,128)S(1)}, f32[88,128]{1,0:T(8,128)S(1)}, u32[]{:S(2)}, u32[]{:S(2)}) collective-permute-start(f32[88,128]{1,0:T(8,128)S(1)} %get-tuple-element.59), channel_id=1, source_target_pairs={{0,4},{1,5},{2,6},{3,7},{4,0},{5,1},{6,2},{7,3},{8,12},{9,13},{10,... | collective-permute-start | bytes 135176 | tf_op jit(solution)/shard_map/ppermute | solution.py:386
  137.3 7.3 %collective-permute-start.21 = (f32[88,128]{1,0:T(8,128)S(1)}, f32[88,128]{1,0:T(8,128)S(1)}, u32[]{:S(2)}, u32[]{:S(2)}) collective-permute-start(f32[88,128]{1,0:T(8,128)S(1)} %get-tuple-element.58), channel_id=1, source_target_pairs={{0,4},{1,5},{2,6},{3,7},{4,0},{5,1},{6,2},{7,3},{8,12},{9,13},{10,... | collective-permute-start | bytes 135176 | tf_op jit(solution)/shard_map/ppermute | solution.py:386
  140.2 6.5 %collective-permute-start.32 = (f32[176,128]{1,0:T(8,128)S(1)}, f32[176,128]{1,0:T(8,128)S(1)}, u32[]{:S(2)}, u32[]{:S(2)}) collective-permute-start(f32[176,128]{1,0:T(8,128)S(1)} %pad_maximum_fusion.8), channel_id=1, source_target_pairs={{0,1},{1,0},{2,3},{3,2},{4,5},{5,4},{6,7},{7,6},{8,9},{9,8},{10,11... | collective-permute-start | bytes 270344 | tf_op jit(solution)/shard_map/ppermute | solution.py:386
  142.2 5.1 %collective-permute-start.12 = (f32[176,128]{1,0:T(8,128)S(1)}, f32[176,128]{1,0:T(8,128)S(1)}, u32[]{:S(2)}, u32[]{:S(2)}) collective-permute-start(f32[176,128]{1,0:T(8,128)S(1)} %pad_maximum_fusion.6), channel_id=1, source_target_pairs={{0,2},{1,3},{2,0},{3,1},{4,6},{5,7},{6,4},{7,5},{8,10},{9,11},{10,... | collective-permute-start | bytes 270344 | tf_op jit(solution)/shard_map/ppermute | solution.py:386
  144.6 4.6 %collective-permute-start.22 = (f32[176,128]{1,0:T(8,128)S(1)}, f32[176,128]{1,0:T(8,128)S(1)}, u32[]{:S(2)}, u32[]{:S(2)}) collective-permute-start(f32[176,128]{1,0:T(8,128)S(1)} %pad_maximum_fusion.7), channel_id=1, source_target_pairs={{0,16},{8,24},{16,0},{24,8},{1,17},{9,25},{17,1},{25,9},{2,18},{10... | collective-permute-start | bytes 270344 | tf_op jit(solution)/shard_map/ppermute | solution.py:386
  146.6 5.6 %collective-permute-start.33 = (f32[352,128]{1,0:T(8,128)S(1)}, f32[352,128]{1,0:T(8,128)S(1)}, u32[]{:S(2)}, u32[]{:S(2)}) collective-permute-start(f32[352,128]{1,0:T(8,128)S(1)} %pad_maximum_fusion.5), channel_id=1, source_target_pairs={{0,16},{8,24},{16,0},{24,8},{1,17},{9,25},{17,1},{25,9},{2,18},{10... | collective-permute-start | bytes 540680 | tf_op jit(solution)/shard_map/ppermute | solution.py:386
  147.3 5.6 %collective-permute-start.13 = (f32[352,128]{1,0:T(8,128)S(1)}, f32[352,128]{1,0:T(8,128)S(1)}, u32[]{:S(2)}, u32[]{:S(2)}) collective-permute-start(f32[352,128]{1,0:T(8,128)S(1)} %pad_maximum_fusion.3), channel_id=1, source_target_pairs={{0,1},{1,0},{2,3},{3,2},{4,5},{5,4},{6,7},{7,6},{8,9},{9,8},{10,11... | collective-permute-start | bytes 540680 | tf_op jit(solution)/shard_map/ppermute | solution.py:386
  149.3 6.5 %collective-permute-start.23 = (f32[352,128]{1,0:T(8,128)S(1)}, f32[352,128]{1,0:T(8,128)S(1)}, u32[]{:S(2)}, u32[]{:S(2)}) collective-permute-start(f32[352,128]{1,0:T(8,128)S(1)} %pad_maximum_fusion.4), channel_id=1, source_target_pairs={{0,2},{1,3},{2,0},{3,1},{4,6},{5,7},{6,4},{7,5},{8,10},{9,11},{10,... | collective-permute-start | bytes 540680 | tf_op jit(solution)/shard_map/ppermute | solution.py:386
  152.2 7.5 %collective-permute-start.34 = (f32[704,128]{1,0:T(8,128)S(1)}, f32[704,128]{1,0:T(8,128)S(1)}, u32[]{:S(2)}, u32[]{:S(2)}) collective-permute-start(f32[704,128]{1,0:T(8,128)S(1)} %pad_maximum_fusion.2.rest_8_), channel_id=1, source_target_pairs={{0,2},{1,3},{2,0},{3,1},{4,6},{5,7},{6,4},{7,5},{8,10},{9,11},{10,... | collective-permute-start | bytes 1081352 | tf_op jit(solution)/shard_map/ppermute | solution.py:386
  152.8 6.9 %collective-permute-start.35 = (f32[704,128]{1,0:T(8,128)S(1)}, f32[704,128]{1,0:T(8,128)S(1)}, u32[]{:S(2)}, u32[]{:S(2)}) collective-permute-start(f32[704,128]{1,0:T(8,128)S(1)} %pad_maximum_fusion.2.rest_8_), channel_id=1, source_target_pairs={{0,8},{8,0},{16,24},{24,16},{1,9},{9,1},{17,25},{25,17},{2,10},{10... | collective-permute-start | bytes 1081352 | tf_op jit(solution)/shard_map/ppermute | solution.py:386
  155.7 8.6 %collective-permute-start.14 = (f32[704,128]{1,0:T(8,128)S(1)}, f32[704,128]{1,0:T(8,128)S(1)}, u32[]{:S(2)}, u32[]{:S(2)}) collective-permute-start(f32[704,128]{1,0:T(8,128)S(1)} %pad_maximum_fusion.rest_0_), channel_id=1, source_target_pairs={{0,16},{8,24},{16,0},{24,8},{1,17},{9,25},{17,1},{25,9},{2,18},{10... | collective-permute-start | bytes 1081352 | tf_op jit(solution)/shard_map/ppermute | solution.py:386
  157.2 8.7 %collective-permute-start.24 = (f32[704,128]{1,0:T(8,128)S(1)}, f32[704,128]{1,0:T(8,128)S(1)}, u32[]{:S(2)}, u32[]{:S(2)}) collective-permute-start(f32[704,128]{1,0:T(8,128)S(1)} %pad_maximum_fusion.1.rest_4_), channel_id=1, source_target_pairs={{0,1},{1,0},{2,3},{3,2},{4,5},{5,4},{6,7},{7,6},{8,9},{9,8},{10,11... | collective-permute-start | bytes 1081352 | tf_op jit(solution)/shard_map/ppermute | solution.py:386
  157.8 8.3 %collective-permute-start.15 = (f32[704,128]{1,0:T(8,128)S(1)}, f32[704,128]{1,0:T(8,128)S(1)}, u32[]{:S(2)}, u32[]{:S(2)}) collective-permute-start(f32[704,128]{1,0:T(8,128)S(1)} %pad_maximum_fusion.rest_0_), channel_id=1, source_target_pairs={{0,8},{8,0},{16,24},{24,16},{1,9},{9,1},{17,25},{25,17},{2,10},{10... | collective-permute-start | bytes 1081352 | tf_op jit(solution)/shard_map/ppermute | solution.py:386
  159.7 6.5 %collective-permute-start.25 = (f32[704,128]{1,0:T(8,128)S(1)}, f32[704,128]{1,0:T(8,128)S(1)}, u32[]{:S(2)}, u32[]{:S(2)}) collective-permute-start(f32[704,128]{1,0:T(8,128)S(1)} %pad_maximum_fusion.1.rest_4_), channel_id=1, source_target_pairs={{0,8},{8,0},{16,24},{24,16},{1,9},{9,1},{17,25},{25,17},{2,10},{10... | collective-permute-start | bytes 1081352 | tf_op jit(solution)/shard_map/ppermute | solution.py:386
  159.8 6.5 %collective-permute-start.36 = (f32[704,128]{1,0:T(8,128)S(1)}, f32[704,128]{1,0:T(8,128)S(1)}, u32[]{:S(2)}, u32[]{:S(2)}) collective-permute-start(f32[704,128]{1,0:T(8,128)S(1)} %collective-permute-done.34.rest_9_), channel_id=1, source_target_pairs={{0,8},{8,0},{16,24},{24,16},{1,9},{9,1},{17,25},{25,17},{2,10},{10... | collective-permute-start | bytes 1081352 | tf_op jit(solution)/shard_map/ppermute | solution.py:386
  (31 other events, 281.7 us)

commit v2 on v1

--- a/solution.py
+++ b/solution.py
@@ -18,14 +18,50 @@
 SMEM = pl.BlockSpec(memory_space=pltpu.SMEM)
 
 
-def dot(left, right):
-    return jnp.dot(left, right, preferred_element_type=jnp.float32)
-
-
-def dot_rows(left, right):
-    return lax.dot_general(
-        left, right, (((0,), (0,)), ((), ())), preferred_element_type=jnp.float32
-    )
+def accumulators(rows, count):
+    return [pltpu.ACC(net)((rows, TILE), jnp.float32) for net in range(2) for i in range(count)]
+
+
+class Pipe:
+    def __init__(self, first, second, accs):
+        count = len(accs) // 2
+        self.accs = (accs[:count], accs[count:])
+        self.tiles = count - 1
+        self.first = first
+        self.second = second
+
+    def push(self, t):
+        t = t % (2 * self.tiles)
+        for net in range(2):
+            if t < self.tiles:
+                tile = self.first[net][:, t * TILE : (t + 1) * TILE]
+            else:
+                t0 = (t - self.tiles) * TILE
+                tile = self.second[net][t0 : t0 + TILE, :]
+            pltpu.matmul_push_rhs(tile, staging_register=t % 2, mxu_index=net)
+
+    def prime(self):
+        self.push(0)
+        self.push(1)
+
+    def run(self, left, act):
+        n = self.tiles
+        for t in range(n):
+            for net in range(2):
+                pltpu.matmul_acc_lhs(self.accs[net][t], left[net], load_staged_rhs=t % 2)
+            self.push(t + 2)
+        for t in range(n, 2 * n):
+            hidden = [act(net, t - n, pltpu.matmul_pop(self.accs[net][t - n])) for net in range(2)]
+            for net in range(2):
+                pltpu.matmul_acc_lhs(self.accs[net][n], hidden[net], load_staged_rhs=t % 2)
+            self.push(t + 2)
+        return [pltpu.matmul_pop(self.accs[net][n]) for net in range(2)]
+
+    def drain(self, left):
+        for net in range(2):
+            for t in range(2):
+                pltpu.matmul_acc_lhs(self.accs[net][t], left, load_staged_rhs=t)
+                pltpu.matmul_pop(self.accs[net][t])
 
 
 def step_copies(own, received, core, half, rows, steps, buffer, sems, k):
@@ -38,12 +74,12 @@
 
 
 def forward_kernel(
+    turn,
     full,
     steps,
     rows,
     info,
     initial,
-    incoming,
     own_noise,
     mate_noise,
     drift_inner,
@@ -56,6 +92,7 @@
     noise_offset,
     *rest,
 ):
+    incoming, rest = (rest[0], rest[1:]) if turn > 0 else (None, rest)
     if full:
         final, states, states_send, q_out, u_out, v_out, a_out = rest[:7]
         noise_buf, in_sems, out_sem, z_buf, q_buf, u_buf, v_buf, a_buf = rest[7:]
@@ -63,7 +100,7 @@
         final, noise_buf, in_sems = rest
     window = 2 * steps
     core = info[0]
-    first = info[1]
+    stage = info[1]
     hidden = drift_inner.shape[1]
 
     def start(k, carry):
@@ -81,9 +118,6 @@
             from_mate.start()
 
         return carry
-
-    lax.fori_loop(0, window, start, 0)
-    begin = jnp.where(first == 1, initial[pl.ds(pl.multiple_of(core * rows, 8), rows), :], incoming[...])
 
     def state_copies(k):
         local = lax.rem(k, steps)
@@ -101,25 +135,29 @@
             for buf, out in ((q_buf, q_out), (u_buf, u_out), (v_buf, v_out), (a_buf, a_out))
         ]
 
-    def body(k, state):
+    def body(pipe, k, carry):
         pltpu.make_async_copy(mate_noise.at[0], noise_buf.at[k], in_sems.at[k]).wait()
+        state = final[...]
         q = state.astype(jnp.bfloat16)
         if full:
             q_buf[k] = q
-        drift = drift_offset[...]
-        spread = noise_offset[...]
-        for j in range(hidden // TILE):
+        saved = (u_buf, v_buf) if full else (None, None)
+
+        def act(net, j, raw):
             cols = slice(j * TILE, (j + 1) * TILE)
-            u = jnp.tanh(dot(q, drift_inner[:, cols]) + drift_hidden[:, cols]).astype(jnp.bfloat16)
-            v = jnp.tanh(dot(q, noise_inner[:, cols]) + noise_hidden[:, cols]).astype(jnp.bfloat16)
+            bias = (drift_hidden, noise_hidden)[net]
+            value = jnp.tanh(raw + bias[:, cols]).astype(jnp.bfloat16)
             if full:
-                u_buf[k, :, cols] = u
-                v_buf[k, :, cols] = v
-            drift = drift + dot(u, drift_outer[cols, :])
-            spread = spread + dot(v, noise_outer[cols, :])
+                saved[net][k, :, cols] = value
+            return value
+
+        drift, spread = pipe.run((q, q), act)
+        drift = drift + drift_offset[...]
+        spread = spread + noise_offset[...]
         s = 0.5 * jnp.tanh(0.5 * spread) + 0.5
         noise = noise_buf[k]
         following = state + delta_time * drift + s * noise
+        final[...] = following
         if full:
             a_buf[k] = noise * s * (1.0 - s)
             z_buf[k] = following
@@ -136,9 +174,23 @@
 
             for copy in saved_copies(k):
                 copy.start()
-        return following
-
-    final[...] = lax.fori_loop(0, window, body, begin)
+        return carry
+
+    def solve(*accs):
+        lax.fori_loop(0, window, start, 0)
+        begin = initial[pl.ds(pl.multiple_of(core * rows, 8), rows), :]
+        if incoming is not None:
+            begin = jnp.where(stage == 0, begin, incoming[...])
+        final[...] = begin
+        pipe = Pipe((drift_inner, noise_inner), (drift_outer, noise_outer), accs)
+        pipe.prime()
+        lax.fori_loop(0, window, functools.partial(body, pipe), 0)
+        pipe.drain(jnp.zeros((rows, TILE), jnp.bfloat16))
+
+    def guarded(*accs):
+        pl.when(stage == turn)(functools.partial(solve, *accs))
+
+    pl.run_scoped(solve if full else guarded, *accumulators(rows, hidden // TILE + 1))
     if full:
 
         def finish(k, carry):
@@ -151,13 +203,14 @@
 
 
 def backward_kernel(
+    turn,
+    stages,
     full,
     steps,
     rows,
     blocks,
     block_rows,
     info,
-    incoming,
     own_cotangent,
     mate_cotangent,
     q_in,
@@ -170,15 +223,17 @@
     noise_outer_t,
     *rest,
 ):
+    incoming, rest = (rest[0], rest[1:]) if turn > 0 else (None, rest)
     if full:
         final, adjoints, adjoints_send, keep_out, send_out = rest[:5]
         (c_buf, u_buf, v_buf, a_buf, in_sems, q_sem, out_sem, q_buf) = rest[5:13]
-        (e_buf, pb_buf, rb_buf, fb_buf, gb_buf, p_sum, r_sum, f_sum, g_sum, packed) = rest[13:]
+        (e_buf, pb_buf, rb_buf, fb_buf, gb_buf, qt_buf) = rest[13:19]
+        (p_sum, r_sum, f_sum, g_sum, packed) = rest[19:]
     else:
         final, c_buf, u_buf, v_buf, a_buf, in_sems = rest
     window = 2 * steps
     core = info[0]
-    last = info[2]
+    stage = info[1]
     width, hidden = drift_outer_t.shape
 
     def saved_copies(k):
@@ -205,13 +260,6 @@
         for copy in saved_copies(k):
             copy.start()
         return carry
-
-    lax.fori_loop(0, window, start, 0)
-    if full:
-        pltpu.make_async_copy(q_in, q_buf, q_sem).start()
-        for ref in (p_sum, r_sum, f_sum, g_sum):
-            ref[...] = jnp.zeros_like(ref)
-    begin = jnp.where(last == 1, jnp.zeros_like(incoming), incoming[...])
 
     def adjoint_copies(k):
         local = lax.rem(k, steps)
@@ -226,37 +274,37 @@
     def partial(x):
         return jnp.sum(x.reshape(rows // 8, 8, x.shape[1]), 0)
 
-    def body(n, adjoint):
+    def body(pipe, n, carry):
         k = window - 1 - n
         pltpu.make_async_copy(mate_cotangent.at[0], c_buf.at[k], in_sems.at[k]).wait()
         for copy in saved_copies(k):
             copy.wait()
-        w = adjoint + c_buf[k]
+        w = final[...] + c_buf[k]
+        final[...] = w
         f = delta_time * w
         g = w * a_buf[k]
         fb = f.astype(jnp.bfloat16)
         gb = g.astype(jnp.bfloat16)
         if full:
-            fb_buf[k] = fb
-            gb_buf[k] = gb
+            fb_buf[:, pl.ds(pl.multiple_of(k * rows, rows), rows)] = fb.T
+            gb_buf[:, pl.ds(pl.multiple_of(k * rows, rows), rows)] = gb.T
+            qt_buf[:, pl.ds(pl.multiple_of(k * rows, rows), rows)] = q_buf[k].T
             f_sum[...] += partial(f)
             g_sum[...] += partial(g)
-        result = w
-        for j in range(hidden // TILE):
+
+        def act(net, j, raw):
             cols = slice(j * TILE, (j + 1) * TILE)
-            u = u_buf[k, :, cols].astype(jnp.float32)
-            v = v_buf[k, :, cols].astype(jnp.float32)
-            p = dot(fb, drift_outer_t[:, cols]) * (1.0 - u * u)
-            r = dot(gb, noise_outer_t[:, cols]) * (1.0 - v * v)
-            pb = p.astype(jnp.bfloat16)
-            rb = r.astype(jnp.bfloat16)
+            value = (u_buf, v_buf)[net][k, :, cols].astype(jnp.float32)
+            back = raw * (1.0 - value * value)
+            low = back.astype(jnp.bfloat16)
             if full:
-                p_sum[:, cols] += partial(p)
-                r_sum[:, cols] += partial(r)
-                pb_buf[k, :, cols] = pb
-                rb_buf[k, :, cols] = rb
-            result = result + dot(pb, drift_inner_t[cols, :])
-            result = result + dot(rb, noise_inner_t[cols, :])
+                (p_sum, r_sum)[net][:, cols] += partial(back)
+                (pb_buf, rb_buf)[net][k, :, cols] = low
+            return low
+
+        drift_part, noise_part = pipe.run((fb, gb), act)
+        result = final[...] + (drift_part + noise_part)
+        final[...] = result
         if full:
             e_buf[k] = result
             mine = k // steps == core
@@ -270,30 +318,73 @@
             def _():
                 send.start()
 
-        return result
-
-    final[...] = lax.fori_loop(0, window, body, begin)
+        return carry
+
+    def solve(*accs):
+        lax.fori_loop(0, window, start, 0)
+        if full:
+            q_copy = pltpu.make_async_copy(q_in, q_buf, q_sem)
+            q_copy.start()
+            for ref in (p_sum, r_sum, f_sum, g_sum):
+                ref[...] = jnp.zeros_like(ref)
+            q_copy.wait()
+        begin = jnp.zeros(final.shape, jnp.float32)
+        if incoming is not None:
+            begin = jnp.where(stage == stages - 1, begin, incoming[...])
+        final[...] = begin
+        pipe = Pipe((drift_outer_t, noise_outer_t), (drift_inner_t, noise_inner_t), accs)
+        pipe.prime()
+        lax.fori_loop(0, window, functools.partial(body, pipe), 0)
+        pipe.drain(jnp.zeros((rows, TILE), jnp.bfloat16))
+
+    def guarded(*accs):
+        pl.when(stage == stages - 1 - turn)(functools.partial(solve, *accs))
+
+    pl.run_scoped(solve if full else guarded, *accumulators(rows, hidden // TILE + 1))
     if not full:
         return
-    pltpu.make_async_copy(q_in, q_buf, q_sem).wait()
     total = window * rows
-    q = q_buf[...].reshape(total, width)
     per_matrix = width * hidden // LANES
-    nets = (
-        (pb_buf, fb_buf, u_buf, p_sum, f_sum),
-        (rb_buf, gb_buf, v_buf, r_sum, g_sum),
-    )
-    for net, (back_buf, low_buf, hid_buf, hidden_sum, offset_sum) in enumerate(nets):
-        low = low_buf[...].reshape(total, width)
-        for j in range(hidden // TILE):
-            cols = slice(j * TILE, (j + 1) * TILE)
-            inner = dot_rows(q, back_buf[:, :, cols].reshape(total, TILE))
-            outer = dot_rows(low, hid_buf[:, :, cols].reshape(total, TILE))
-            for i in range(TILE // LANES):
-                row = (j * (TILE // LANES) + i) * width
-                lanes = slice(i * LANES, (i + 1) * LANES)
-                packed[net, row : row + width, :] = inner[:, lanes]
-                packed[net, per_matrix + row : per_matrix + row + width, :] = outer[:, lanes]
+    lefts = ((qt_buf, fb_buf), (qt_buf, gb_buf))
+    rights = ((pb_buf, u_buf), (rb_buf, v_buf))
+
+    def products(*accs):
+        per_step = TILE // rows
+        chain = [
+            (j, which, c)
+            for j in range(hidden // TILE)
+            for which in range(2)
+            for c in range(total // TILE)
+        ]
+
+        def push(n):
+            j, which, c = chain[n]
+            for net in range(2):
+                block = rights[net][which][
+                    c * per_step : (c + 1) * per_step, :, j * TILE : (j + 1) * TILE
+                ]
+                pltpu.matmul_push_rhs(
+                    block.reshape(TILE, TILE), staging_register=n % 2, mxu_index=net
+                )
+
+        push(0)
+        push(1)
+        for n, (j, which, c) in enumerate(chain):
+            slot = (2 * j + which) % 4
+            for net in range(2):
+                left = lefts[net][which][:, c * TILE : (c + 1) * TILE]
+                pltpu.matmul_acc_lhs(accs[4 * net + slot], left, load_staged_rhs=n % 2)
+            if n + 2 < len(chain):
+                push(n + 2)
+            if c == total // TILE - 1:
+                for net in range(2):
+                    grad = pltpu.matmul_pop(accs[4 * net + slot])
+                    for i in range(TILE // LANES):
+                        row = which * per_matrix + (j * (TILE // LANES) + i) * width
+                        packed[net, row : row + width, :] = grad[:, i * LANES : (i + 1) * LANES]
+
+    pl.run_scoped(products, *accumulators(width, 4))
+    for net, (hidden_sum, offset_sum) in enumerate(((p_sum, f_sum), (r_sum, g_sum))):
         base = 2 * per_matrix
         hidden_total = jnp.sum(hidden_sum[...], 0, keepdims=True)
         offset_total = jnp.sum(offset_sum[...], 0, keepdims=True)
@@ -307,7 +398,7 @@
     def grad_copies(out, net):
         copies = []
         for color in range(COLORS):
-            me = info[3 + color]
+            me = info[2 + color]
             for s in range(blocks):
                 source = (color * blocks + s) * block_rows
                 place = color * blocks + ((s ^ (blocks - 1)) ^ me)
@@ -340,7 +431,7 @@
     half = blocks // 2
     copies = []
     for color in range(COLORS):
-        me = info[3 + color]
+        me = info[2 + color]
         for side in range(2):
             net = core if side == 0 else 1 - core
             for top in range(2):
@@ -439,10 +530,7 @@
             place = 2 * place + (index // bit) % 2
         return place
 
-    info = jnp.stack(
-        [core, (stage == 0).astype(jnp.int32), (stage == stages - 1).astype(jnp.int32)]
-        + [position(order) for order in orders]
-    ).astype(jnp.int32)
+    info = jnp.stack([core, stage] + [position(order) for order in orders]).astype(jnp.int32)
 
     def other_half(array):
         return lax.dynamic_slice_in_dim(array, (1 - core) * rows, rows, 1)
@@ -464,7 +552,7 @@
     def sds(shape, dtype=f32):
         return jax.ShapeDtypeStruct(shape, dtype)
 
-    def forward(incoming, full):
+    def forward(incoming, turn, full):
         out_shape = [sds((rows, width))]
         out_specs = [VMEM]
         scratch = [
@@ -490,22 +578,28 @@
                 pltpu.VMEM((window, rows, width), f32),
             ]
         return pl.pallas_call(
-            functools.partial(forward_kernel, full, steps, rows),
+            functools.partial(forward_kernel, turn, full, steps, rows),
             out_shape=out_shape,
-            in_specs=[SMEM, VMEM, VMEM, ANY, ANY] + [VMEM] * 8,
+            in_specs=[SMEM, VMEM, ANY, ANY] + [VMEM] * (8 + (turn > 0)),
             out_specs=out_specs,
             scratch_shapes=scratch,
             compiler_params=PARAMS,
             name="forward_full" if full else "forward_light",
-        )(info, initial_state, incoming, increments, mate_noise, *weights)
-
-    incoming = jnp.zeros((rows, width), f32)
-    for turn_index in range(stages - 1):
-        incoming = moved(forward(incoming, False)[0], 2)
-    unused, states, states_send, q, u, v, a = forward(incoming, True)
+        )(info, initial_state, increments, mate_noise, *weights, *incoming)
+
+    def relay(run, distance, reached):
+        incoming = ()
+        for turn in range(stages - 1):
+            arrived = moved(run(incoming, turn, False)[0], distance)
+            if turn > 0:
+                arrived = jnp.where(reached == turn + 1, arrived, incoming[0])
+            incoming = (arrived,)
+        return run(incoming, stages - 1, True)
+
+    unused, states, states_send, q, u, v, a = relay(forward, 2, stage)
     states_mate = flipped(states_send, "tm", 1)
 
-    def backward(incoming, full):
+    def backward(incoming, turn, full):
         out_shape = [sds((rows, width))]
         out_specs = [VMEM]
         scratch = [
@@ -530,8 +624,9 @@
                 pltpu.VMEM((window, rows, width), f32),
                 pltpu.VMEM((window, rows, hidden), bf16),
                 pltpu.VMEM((window, rows, hidden), bf16),
-                pltpu.VMEM((window, rows, width), bf16),
-                pltpu.VMEM((window, rows, width), bf16),
+                pltpu.VMEM((width, window * rows), bf16),
+                pltpu.VMEM((width, window * rows), bf16),
+                pltpu.VMEM((width, window * rows), bf16),
                 pltpu.VMEM((8, hidden), f32),
                 pltpu.VMEM((8, hidden), f32),
                 pltpu.VMEM((8, width), f32),
@@ -539,19 +634,18 @@
                 pltpu.VMEM((2, packed_rows, LANES), f32),
             ]
         return pl.pallas_call(
-            functools.partial(backward_kernel, full, steps, rows, blocks, block_rows),
+            functools.partial(
+                backward_kernel, turn, stages, full, steps, rows, blocks, block_rows
+            ),
             out_shape=out_shape,
-            in_specs=[SMEM, VMEM] + [ANY] * 6 + [VMEM] * 4,
+            in_specs=[SMEM] + [ANY] * 6 + [VMEM] * (4 + (turn > 0)),
             out_specs=out_specs,
             scratch_shapes=scratch,
             compiler_params=PARAMS,
             name="backward_full" if full else "backward_light",
-        )(info, incoming, cotangents, mate_cotangent, q, u, v, a, *turned)
-
-    incoming = jnp.zeros((rows, width), f32)
-    for turn_index in range(stages - 1):
-        incoming = moved(backward(incoming, False)[0], -2)
-    unused, adjoints, adjoints_send, keep, send = backward(incoming, True)
+        )(info, cotangents, mate_cotangent, q, u, v, a, *turned, *incoming)
+
+    unused, adjoints, adjoints_send, keep, send = relay(backward, -2, stages - 1 - stage)
     mate_grads = flipped(send, "tm", 1)
     adjoints_mate = flipped(adjoints_send, "tm", 1)
 

time: 175 us -> 161 us (0.920)
  Pallas kernels: 73.8 us -> 53.3 us
  waiting for transfers between devices: 45.7 us -> 55.3 us
  starting transfers between devices: 38.4 us -> 35.6 us
    pallas_call x4, Pallas kernels: 68 us -> 47.5 us  [the longest x2 25.6 us: backward(): pl.pallas_call(functools.partial(backward_kernel, turn, stages, full, ste...]
    ppermute x2, waiting for transfers between devices: 5.87 us -> 15.2 us  [moved(): lax.ppermute(block, 'tm', [(i, i + distance) for i in range(count) if 0 <...]
    ppermute x2, starting transfers between devices: 6.36 us -> 2.9 us  [moved(): lax.ppermute(block, 'tm', [(i, i + distance) for i in range(count) if 0 <...]
  transfers between devices with their start and end apart: 37 -> 37, of which waited for: 20 -> 20; matrix products, arithmetic and copies ran while one was open for 4% -> 4% of each run, Pallas kernels for 21% -> 14%
where the time goes in v2:
time: 161 us; the launch traced here: 160 us
  waiting for transfers between devices  55.3 us (34%)
  Pallas kernels  53.3 us (33%)
  starting transfers between devices  35.6 us (22%)
  local copies, waits for them, and re-layouts  13.2 us (8%)
  other arithmetic  1.8 us (1%)
    ppermute x35, waiting for transfers between devices, flipped(): lax.ppermute(block, axis, [(i, i ^ bit) for i in range(lax.axis_size(axis...  40.1 us
    ppermute x35, starting transfers between devices, flipped(): lax.ppermute(block, axis, [(i, i ^ bit) for i in range(lax.axis_size(axis...  32.7 us
    pallas_call x2, Pallas kernels, backward(): pl.pallas_call(functools.partial(backward_kernel, turn, stages, full, ste...  25.6 us
    pallas_call x2, Pallas kernels, forward(): pl.pallas_call(functools.partial(forward_kernel, turn, full, steps, rows)...  21.9 us
    ppermute x2, waiting for transfers between devices, moved(): lax.ppermute(block, 'tm', [(i, i + distance) for i in range(count) if 0 <...  15.2 us
    unnamed x56, local copies, waits for them, and re-layouts  8.92 us
    pallas_call x1, Pallas kernels, shards(): pl.pallas_call(functools.partial(finish_kernel, blocks, block_rows, width...  5.79 us
    dynamic_slice x2, local copies, waits for them, and re-layouts, other_half(): return lax.dynamic_slice_in_dim(array, (1 - core) * rows, rows, 1)  3.5 us
  transfers between devices with their start and end apart: 37, of which 20 were waited for; matrix products, arithmetic and copies ran while one was open for 4% of the time, Pallas kernels for 14%

profile of v2, /device:TPU:0, one launch (start us, length us, event | category | flops | bytes accessed | tf_op | source)
XLA Modules:
  0.0 160.3 jit_solution(13712272854871581272)
XLA Ops:
  0.7 2.4 %constant_dynamic-slice_fusion.1 = f32[8,128,256]{2,1,0:T(8,128)} fusion(f32[8,256,256]{2,1,0:T(8,128)} %own_noise.3, s32[]{:T(128)S(6)} %select_n.73), kind=kLoop, calls=%fused_computation.57 | loop fusion | bytes 2097156 | tf_op jit(solution)/shard_map/dynamic_slice | solution.py:536
  6.2 10.5 %forward_light.1 = f32[128,256]{1,0:T(8,128)} custom-call(s32[5]{0:T(128)} %stack.23.info, f32[256,256]{1,0:T(8,128)} %initial.3, f32[8,256,256]{2,1,0:T(8,128)} %own_noise.3, f32[8,128,256]{2,1,0:T(8,128)} %collective-permute-done.mate_noise, bf16[256,1024]{1,0:T(8,128)(2,1)} %drift_inner.3, f32[1,1024]{1,0:T(1,128)} %bitcast.25, ...), custom_call_target="tpu_custom_call" | custom-call | tf_op jit(solution)/shard_map/forward_light/pallas_call | solution.py:580
  16.8 1.4 collective-permute-start.1
  22.9 11.4 %forward_full.1 = (f32[128,256]{1,0:T(8,128)}, f32[8,256,256]{2,1,0:T(8,128)}, f32[8,128,256]{2,1,0:T(8,128)}, bf16[16,128,256]{2,1,0:T(8,128)(2,1)}, bf16[16,12...) custom-call(s32[5]{0:T(128)} %stack.23.info, f32[256,256]{1,0:T(8,128)} %initial.3, ...), custom_call_target="tpu_custom_call" | custom-call | tf_op jit(solution)/shard_map/forward_full/pallas_call | solution.py:580
  35.3 2.3 %backward_light.1 = f32[128,256]{1,0:T(8,128)} custom-call(s32[5]{0:T(128)} %stack.23.info, f32[8,256,256]{2,1,0:T(8,128)} %own_cotangent.3, f32[8,128,256]{2,1,0:T(8,128)} %copy-done.5, bf16[16,128,256]{2,1,0:T(8,128)(2,1)} %get-tuple-element.30.q_in, bf16[16,128,1024]{2,1,0:T(8,128)(2,1)} %get-tuple-element.31.u_in, ...), custom_call_target="tpu_custom_call" | custom-call | tf_op jit(solution)/shard_map/backward_light/pallas_call | solution.py:636
  37.7 1.5 collective-permute-start.4
  39.2 15.2 %collective-permute-done.4.rest_0_ = f32[128,256]{1,0:T(8,128)S(1)} collective-permute-done((f32[128,256]{1,0:T(8,128)}, f32[128,256]{1,0:T(8,128)S(1)}, u32[]{:S(2)}, u32[]{:S(2)}) %collective-permute-start.4) | collective-permute-done | bytes 131104 | tf_op jit(solution)/shard_map/ppermute | solution.py:482
  55.0 23.2 %backward_full.1 = (f32[128,256]{1,0:T(8,128)}, f32[8,256,256]{2,1,0:T(8,128)}, f32[8,128,256]{2,1,0:T(8,128)}, f32[4224,128]{1,0:T(8,128)}, f32[4224,128]{1,0:T(8,128)}) custom-call(s32[5]{0:T(128)} %stack.23.info, f32[8,256,256]{2,1,0:T(8,128)} %own_cotangent.3, f32[8,128,256]{2,1,0:T(8,128)} %copy-done.5, bf16[16,128,256]{2,1,0:T(8,128)(2,1)} %get-tuple-element.30.q_in, ...), custom_call_target="tpu_custom_call" | custom-call | tf_op jit(solution)/shard_map/backward_full/pallas_call | solution.py:636
  78.4 4.5 %collective-permute-done.6 = f32[4224,128]{1,0:T(8,128)S(1)} collective-permute-done((f32[4224,128]{1,0:T(8,128)}, f32[4224,128]{1,0:T(8,128)S(1)}, u32[]{:S(2)}, u32[]{:S(2)}) %collective-permute-start.6) | collective-permute-done | bytes 2162720 | tf_op jit(solution)/shard_map/ppermute | solution.py:477
  82.8 1.3 slice_add_fusion
  84.1 2.5 %collective-permute-start.27 = (f32[704,128]{1,0:T(8,128)S(1)}, f32[704,128]{1,0:T(8,128)S(1)}, u32[]{:S(2)}, u32[]{:S(2)}) collective-permute-start(f32[704,128]{1,0:T(8,128)S(1)} %get-tuple-element.55), channel_id=1, source_target_pairs={{0,2},{1,3},{2,0},{3,1},{4,6},{5,7},{6,4},{7,5},{8,10},{9,11},{10,... | collective-permute-start | bytes 1081352 | tf_op jit(solution)/shard_map/ppermute | solution.py:477
  86.6 1.5 collective-permute-start.17
  88.2 7.2 %collective-permute-done.27 = f32[704,128]{1,0:T(8,128)S(1)} collective-permute-done((f32[704,128]{1,0:T(8,128)S(1)}, f32[704,128]{1,0:T(8,128)S(1)}, u32[]{:S(2)}, u32[]{:S(2)}) %collective-permute-start.27) | collective-permute-done | bytes 360480 | tf_op jit(solution)/shard_map/ppermute | solution.py:477
  95.3 1.5 collective-permute-done.17
  99.4 4.4 %collective-permute-done.28 = f32[352,128]{1,0:T(8,128)S(1)} collective-permute-done((f32[352,128]{1,0:T(8,128)S(1)}, f32[352,128]{1,0:T(8,128)S(1)}, u32[]{:S(2)}, u32[]{:S(2)}) %collective-permute-start.28) | collective-permute-done | bytes 180256 | tf_op jit(solution)/shard_map/ppermute | solution.py:477
  105.0 1.7 %collective-permute-start.19 = (f32[176,128]{1,0:T(8,128)S(1)}, f32[176,128]{1,0:T(8,128)S(1)}, u32[]{:S(2)}, u32[]{:S(2)}) collective-permute-start(f32[176,128]{1,0:T(8,128)S(1)} %get-tuple-element.50), channel_id=1, source_target_pairs={{0,16},{8,24},{16,0},{24,8},{1,17},{9,25},{17,1},{25,9},{2,18},{10... | collective-permute-start | bytes 270344 | tf_op jit(solution)/shard_map/ppermute | solution.py:477
  106.8 1.7 %collective-permute-start.9 = (f32[176,128]{1,0:T(8,128)S(1)}, f32[176,128]{1,0:T(8,128)S(1)}, u32[]{:S(2)}, u32[]{:S(2)}) collective-permute-start(f32[176,128]{1,0:T(8,128)S(1)} %get-tuple-element.51), channel_id=1, source_target_pairs={{0,2},{1,3},{2,0},{3,1},{4,6},{5,7},{6,4},{7,5},{8,10},{9,11},{10,... | collective-permute-start | bytes 270344 | tf_op jit(solution)/shard_map/ppermute | solution.py:477
  109.2 2.7 %collective-permute-start.30 = (f32[88,128]{1,0:T(8,128)S(1)}, f32[88,128]{1,0:T(8,128)S(1)}, u32[]{:S(2)}, u32[]{:S(2)}) collective-permute-start(f32[88,128]{1,0:T(8,128)S(1)} %slice_add_fusion.18), channel_id=1, source_target_pairs={{0,4},{1,5},{2,6},{3,7},{4,0},{5,1},{6,2},{7,3},{8,12},{9,13},{10,... | collective-permute-start | bytes 135176 | tf_op jit(solution)/shard_map/ppermute | solution.py:477
  111.8 2.3 %collective-permute-done.30 = f32[88,128]{1,0:T(8,128)S(1)} collective-permute-done((f32[88,128]{1,0:T(8,128)S(1)}, f32[88,128]{1,0:T(8,128)S(1)}, u32[]{:S(2)}, u32[]{:S(2)}) %collective-permute-start.30) | collective-permute-done | bytes 45088 | tf_op jit(solution)/shard_map/ppermute | solution.py:477
  114.2 3.1 %collective-permute-start.20 = (f32[88,128]{1,0:T(8,128)S(1)}, f32[88,128]{1,0:T(8,128)S(1)}, u32[]{:S(2)}, u32[]{:S(2)}) collective-permute-start(f32[88,128]{1,0:T(8,128)S(1)} %get-tuple-element.47), channel_id=1, source_target_pairs={{0,4},{1,5},{2,6},{3,7},{4,0},{5,1},{6,2},{7,3},{8,12},{9,13},{10,... | collective-permute-start | bytes 135176 | tf_op jit(solution)/shard_map/ppermute | solution.py:477
  118.0 2.8 %collective-permute-start.31 = (f32[88,128]{1,0:T(8,128)S(1)}, f32[88,128]{1,0:T(8,128)S(1)}, u32[]{:S(2)}, u32[]{:S(2)}) collective-permute-start(f32[88,128]{1,0:T(8,128)S(1)} %get-tuple-element.46), channel_id=1, source_target_pairs={{0,4},{1,5},{2,6},{3,7},{4,0},{5,1},{6,2},{7,3},{8,12},{9,13},{10,... | collective-permute-start | bytes 135176 | tf_op jit(solution)/shard_map/ppermute | solution.py:477
  120.8 1.9 %collective-permute-done.10 = f32[88,128]{1,0:T(8,128)S(1)} collective-permute-done((f32[88,128]{1,0:T(8,128)S(1)}, f32[88,128]{1,0:T(8,128)S(1)}, u32[]{:S(2)}, u32[]{:S(2)}) %collective-permute-start.10) | collective-permute-done | bytes 45088 | tf_op jit(solution)/shard_map/ppermute | solution.py:477
  122.9 2.8 %collective-permute-start.21 = (f32[88,128]{1,0:T(8,128)S(1)}, f32[88,128]{1,0:T(8,128)S(1)}, u32[]{:S(2)}, u32[]{:S(2)}) collective-permute-start(f32[88,128]{1,0:T(8,128)S(1)} %get-tuple-element.58), channel_id=1, source_target_pairs={{0,4},{1,5},{2,6},{3,7},{4,0},{5,1},{6,2},{7,3},{8,12},{9,13},{10,... | collective-permute-start | bytes 135176 | tf_op jit(solution)/shard_map/ppermute | solution.py:477
  127.8 2.4 %collective-permute-start.12 = (f32[176,128]{1,0:T(8,128)S(1)}, f32[176,128]{1,0:T(8,128)S(1)}, u32[]{:S(2)}, u32[]{:S(2)}) collective-permute-start(f32[176,128]{1,0:T(8,128)S(1)} %pad_maximum_fusion.6), channel_id=1, source_target_pairs={{0,2},{1,3},{2,0},{3,1},{4,6},{5,7},{6,4},{7,5},{8,10},{9,11},{10,... | collective-permute-start | bytes 270344 | tf_op jit(solution)/shard_map/ppermute | solution.py:477
  130.2 2.0 %collective-permute-start.22 = (f32[176,128]{1,0:T(8,128)S(1)}, f32[176,128]{1,0:T(8,128)S(1)}, u32[]{:S(2)}, u32[]{:S(2)}) collective-permute-start(f32[176,128]{1,0:T(8,128)S(1)} %pad_maximum_fusion.7), channel_id=1, source_target_pairs={{0,16},{8,24},{16,0},{24,8},{1,17},{9,25},{17,1},{25,9},{2,18},{10... | collective-permute-start | bytes 270344 | tf_op jit(solution)/shard_map/ppermute | solution.py:477
  136.1 1.7 %collective-permute-done.33 = f32[352,128]{1,0:T(8,128)S(1)} collective-permute-done((f32[352,128]{1,0:T(8,128)S(1)}, f32[352,128]{1,0:T(8,128)S(1)}, u32[]{:S(2)}, u32[]{:S(2)}) %collective-permute-start.33) | collective-permute-done | bytes 180256 | tf_op jit(solution)/shard_map/ppermute | solution.py:477
  138.5 2.8 %collective-permute-done.23 = f32[352,128]{1,0:T(8,128)S(1)} collective-permute-done((f32[352,128]{1,0:T(8,128)S(1)}, f32[352,128]{1,0:T(8,128)S(1)}, u32[]{:S(2)}, u32[]{:S(2)}) %collective-permute-start.23) | collective-permute-done | bytes 180256 | tf_op jit(solution)/shard_map/ppermute | solution.py:477
  141.3 1.4 collective-permute-start.14
  143.4 1.9 %collective-permute-done.34.rest_9_ = f32[704,128]{1,0:T(8,128)S(1)} collective-permute-done((f32[704,128]{1,0:T(8,128)S(1)}, f32[704,128]{1,0:T(8,128)S(1)}, u32[]{:S(2)}, u32[]{:S(2)}) %collective-permute-start.34) | collective-permute-done | bytes 360480 | tf_op jit(solution)/shard_map/ppermute | solution.py:477
  145.8 4.1 %collective-permute-done.14.rest_1_ = f32[704,128]{1,0:T(8,128)S(1)} collective-permute-done((f32[704,128]{1,0:T(8,128)S(1)}, f32[704,128]{1,0:T(8,128)S(1)}, u32[]{:S(2)}, u32[]{:S(2)}) %collective-permute-start.14) | collective-permute-done | bytes 360480 | tf_op jit(solution)/shard_map/ppermute | solution.py:477
  149.9 1.6 collective-permute-done.24.rest_5_
  154.4 5.8 %finish.1 = (f32[256,1024]{1,0:T(8,128)}, f32[1,1024]{1,0:T(1,128)}, f32[1024,256]{1,0:T(8,128)}, f32[1,256]{1,0:T(1,128)}, f32[256,1024]{1,0:T(8,128)}, /*index...) custom-call(s32[5]{0:T(128)} %stack.23.info, f32[704,128]{1,0:T(8,128)} %copy-done.8, f32[704,128]{1,0:T(8,128)} %copy-done.12, ...), custom_call_target="tpu_custom_call" | custom-call | tf_op jit(solution)/shard_map/finish/pallas_call | solution.py:682
  (123 shorter events, 25.5 us)
Async XLA Ops:
  4.7 29.7 %collective-permute-start.3 = (f32[8,128,256]{2,1,0:T(8,128)}, f32[8,128,256]{2,1,0:T(8,128)S(1)}, u32[]{:S(2)}, u32[]{:S(2)}) collective-permute-start(f32[8,128,256]{2,1,0:T(8,128)} %constant_dynamic-slice_fusion), channel_id=1, source_target_pairs={{0,8},{8,0},{16,24},{24,16},{1,9},{9,1},{17,25},{25,17},{2,10},{10... | collective-permute-start | bytes 3145736 | tf_op jit(solution)/shard_map/ppermute | solution.py:477
  16.8 5.5 %collective-permute-start.1 = (f32[128,256]{1,0:T(8,128)}, f32[128,256]{1,0:T(8,128)S(1)}, u32[]{:S(2)}, u32[]{:S(2)}) collective-permute-start(f32[128,256]{1,0:T(8,128)} %forward_light.1), channel_id=1, source_target_pairs={{0,16},{8,24},{1,17},{9,25},{2,18},{10,26},{3,19},{11,27},{4,20},{... | collective-permute-start | bytes 393224 | tf_op jit(solution)/shard_map/ppermute | solution.py:482
  37.7 16.7 %collective-permute-start.4 = (f32[128,256]{1,0:T(8,128)}, f32[128,256]{1,0:T(8,128)S(1)}, u32[]{:S(2)}, u32[]{:S(2)}) collective-permute-start(f32[128,256]{1,0:T(8,128)} %backward_light.1), channel_id=1, source_target_pairs={{16,0},{24,8},{17,1},{25,9},{18,2},{26,10},{19,3},{27,11},{20,4},{... | collective-permute-start | bytes 393224 | tf_op jit(solution)/shard_map/ppermute | solution.py:482
  84.1 11.2 %collective-permute-start.27 = (f32[704,128]{1,0:T(8,128)S(1)}, f32[704,128]{1,0:T(8,128)S(1)}, u32[]{:S(2)}, u32[]{:S(2)}) collective-permute-start(f32[704,128]{1,0:T(8,128)S(1)} %get-tuple-element.55), channel_id=1, source_target_pairs={{0,2},{1,3},{2,0},{3,1},{4,6},{5,7},{6,4},{7,5},{8,10},{9,11},{10,... | collective-permute-start | bytes 1081352 | tf_op jit(solution)/shard_map/ppermute | solution.py:477
  86.6 10.2 %collective-permute-start.17 = (f32[704,128]{1,0:T(8,128)S(1)}, f32[704,128]{1,0:T(8,128)S(1)}, u32[]{:S(2)}, u32[]{:S(2)}) collective-permute-start(f32[704,128]{1,0:T(8,128)S(1)} %get-tuple-element.56), channel_id=1, source_target_pairs={{0,1},{1,0},{2,3},{3,2},{4,5},{5,4},{6,7},{7,6},{8,9},{9,8},{10,11... | collective-permute-start | bytes 1081352 | tf_op jit(solution)/shard_map/ppermute | solution.py:477
  88.2 9.9 %collective-permute-start.7 = (f32[704,128]{1,0:T(8,128)S(1)}, f32[704,128]{1,0:T(8,128)S(1)}, u32[]{:S(2)}, u32[]{:S(2)}) collective-permute-start(f32[704,128]{1,0:T(8,128)S(1)} %get-tuple-element.57), channel_id=1, source_target_pairs={{0,16},{8,24},{16,0},{24,8},{1,17},{9,25},{17,1},{25,9},{2,18},{10... | collective-permute-start | bytes 1081352 | tf_op jit(solution)/shard_map/ppermute | solution.py:477
  98.2 5.6 %collective-permute-start.28 = (f32[352,128]{1,0:T(8,128)S(1)}, f32[352,128]{1,0:T(8,128)S(1)}, u32[]{:S(2)}, u32[]{:S(2)}) collective-permute-start(f32[352,128]{1,0:T(8,128)S(1)} %get-tuple-element.52), channel_id=1, source_target_pairs={{0,16},{8,24},{16,0},{24,8},{1,17},{9,25},{17,1},{25,9},{2,18},{10... | collective-permute-start | bytes 540680 | tf_op jit(solution)/shard_map/ppermute | solution.py:477
  98.5 5.5 %collective-permute-start.18 = (f32[352,128]{1,0:T(8,128)S(1)}, f32[352,128]{1,0:T(8,128)S(1)}, u32[]{:S(2)}, u32[]{:S(2)}) collective-permute-start(f32[352,128]{1,0:T(8,128)S(1)} %get-tuple-element.53), channel_id=1, source_target_pairs={{0,2},{1,3},{2,0},{3,1},{4,6},{5,7},{6,4},{7,5},{8,10},{9,11},{10,... | collective-permute-start | bytes 540680 | tf_op jit(solution)/shard_map/ppermute | solution.py:477
  99.0 5.5 %collective-permute-start.8 = (f32[352,128]{1,0:T(8,128)S(1)}, f32[352,128]{1,0:T(8,128)S(1)}, u32[]{:S(2)}, u32[]{:S(2)}) collective-permute-start(f32[352,128]{1,0:T(8,128)S(1)} %get-tuple-element.54), channel_id=1, source_target_pairs={{0,1},{1,0},{2,3},{3,2},{4,5},{5,4},{6,7},{7,6},{8,9},{9,8},{10,11... | collective-permute-start | bytes 540680 | tf_op jit(solution)/shard_map/ppermute | solution.py:477
  105.0 6.8 %collective-permute-start.19 = (f32[176,128]{1,0:T(8,128)S(1)}, f32[176,128]{1,0:T(8,128)S(1)}, u32[]{:S(2)}, u32[]{:S(2)}) collective-permute-start(f32[176,128]{1,0:T(8,128)S(1)} %get-tuple-element.50), channel_id=1, source_target_pairs={{0,16},{8,24},{16,0},{24,8},{1,17},{9,25},{17,1},{25,9},{2,18},{10... | collective-permute-start | bytes 270344 | tf_op jit(solution)/shard_map/ppermute | solution.py:477
  106.8 5.0 %collective-permute-start.9 = (f32[176,128]{1,0:T(8,128)S(1)}, f32[176,128]{1,0:T(8,128)S(1)}, u32[]{:S(2)}, u32[]{:S(2)}) collective-permute-start(f32[176,128]{1,0:T(8,128)S(1)} %get-tuple-element.51), channel_id=1, source_target_pairs={{0,2},{1,3},{2,0},{3,1},{4,6},{5,7},{6,4},{7,5},{8,10},{9,11},{10,... | collective-permute-start | bytes 270344 | tf_op jit(solution)/shard_map/ppermute | solution.py:477
  109.2 5.0 %collective-permute-start.30 = (f32[88,128]{1,0:T(8,128)S(1)}, f32[88,128]{1,0:T(8,128)S(1)}, u32[]{:S(2)}, u32[]{:S(2)}) collective-permute-start(f32[88,128]{1,0:T(8,128)S(1)} %slice_add_fusion.18), channel_id=1, source_target_pairs={{0,4},{1,5},{2,6},{3,7},{4,0},{5,1},{6,2},{7,3},{8,12},{9,13},{10,... | collective-permute-start | bytes 135176 | tf_op jit(solution)/shard_map/ppermute | solution.py:477
  114.2 6.6 %collective-permute-start.20 = (f32[88,128]{1,0:T(8,128)S(1)}, f32[88,128]{1,0:T(8,128)S(1)}, u32[]{:S(2)}, u32[]{:S(2)}) collective-permute-start(f32[88,128]{1,0:T(8,128)S(1)} %get-tuple-element.47), channel_id=1, source_target_pairs={{0,4},{1,5},{2,6},{3,7},{4,0},{5,1},{6,2},{7,3},{8,12},{9,13},{10,... | collective-permute-start | bytes 135176 | tf_op jit(solution)/shard_map/ppermute | solution.py:477
  117.4 5.3 %collective-permute-start.10 = (f32[88,128]{1,0:T(8,128)S(1)}, f32[88,128]{1,0:T(8,128)S(1)}, u32[]{:S(2)}, u32[]{:S(2)}) collective-permute-start(f32[88,128]{1,0:T(8,128)S(1)} %get-tuple-element.48), channel_id=1, source_target_pairs={{0,4},{1,5},{2,6},{3,7},{4,0},{5,1},{6,2},{7,3},{8,12},{9,13},{10,... | collective-permute-start | bytes 135176 | tf_op jit(solution)/shard_map/ppermute | solution.py:477
  117.5 25.3 %collective-permute-start.2 = (f32[8,128,256]{2,1,0:T(8,128)S(1)}, f32[8,128,256]{2,1,0:T(8,128)S(1)}, u32[]{:S(2)}, u32[]{:S(2)}) collective-permute-start(f32[8,128,256]{2,1,0:T(8,128)S(1)} %copy-done.24), channel_id=1, source_target_pairs={{0,8},{8,0},{16,24},{24,16},{1,9},{9,1},{17,25},{25,17},{2,10},{10... | collective-permute-start | bytes 3145736 | tf_op jit(solution)/shard_map/ppermute | solution.py:477
  117.5 26.0 %collective-permute-start.5 = (f32[8,128,256]{2,1,0:T(8,128)S(1)}, f32[8,128,256]{2,1,0:T(8,128)S(1)}, u32[]{:S(2)}, u32[]{:S(2)}) collective-permute-start(f32[8,128,256]{2,1,0:T(8,128)S(1)} %copy-done.25), channel_id=1, source_target_pairs={{0,8},{8,0},{16,24},{24,16},{1,9},{9,1},{17,25},{25,17},{2,10},{10... | collective-permute-start | bytes 3145736 | tf_op jit(solution)/shard_map/ppermute | solution.py:477
  118.0 7.8 %collective-permute-start.31 = (f32[88,128]{1,0:T(8,128)S(1)}, f32[88,128]{1,0:T(8,128)S(1)}, u32[]{:S(2)}, u32[]{:S(2)}) collective-permute-start(f32[88,128]{1,0:T(8,128)S(1)} %get-tuple-element.46), channel_id=1, source_target_pairs={{0,4},{1,5},{2,6},{3,7},{4,0},{5,1},{6,2},{7,3},{8,12},{9,13},{10,... | collective-permute-start | bytes 135176 | tf_op jit(solution)/shard_map/ppermute | solution.py:477
  122.8 5.0 %collective-permute-start.11 = (f32[88,128]{1,0:T(8,128)S(1)}, f32[88,128]{1,0:T(8,128)S(1)}, u32[]{:S(2)}, u32[]{:S(2)}) collective-permute-start(f32[88,128]{1,0:T(8,128)S(1)} %get-tuple-element.59), channel_id=1, source_target_pairs={{0,4},{1,5},{2,6},{3,7},{4,0},{5,1},{6,2},{7,3},{8,12},{9,13},{10,... | collective-permute-start | bytes 135176 | tf_op jit(solution)/shard_map/ppermute | solution.py:477
  122.9 7.3 %collective-permute-start.21 = (f32[88,128]{1,0:T(8,128)S(1)}, f32[88,128]{1,0:T(8,128)S(1)}, u32[]{:S(2)}, u32[]{:S(2)}) collective-permute-start(f32[88,128]{1,0:T(8,128)S(1)} %get-tuple-element.58), channel_id=1, source_target_pairs={{0,4},{1,5},{2,6},{3,7},{4,0},{5,1},{6,2},{7,3},{8,12},{9,13},{10,... | collective-permute-start | bytes 135176 | tf_op jit(solution)/shard_map/ppermute | solution.py:477
  125.8 6.5 %collective-permute-start.32 = (f32[176,128]{1,0:T(8,128)S(1)}, f32[176,128]{1,0:T(8,128)S(1)}, u32[]{:S(2)}, u32[]{:S(2)}) collective-permute-start(f32[176,128]{1,0:T(8,128)S(1)} %pad_maximum_fusion.8), channel_id=1, source_target_pairs={{0,1},{1,0},{2,3},{3,2},{4,5},{5,4},{6,7},{7,6},{8,9},{9,8},{10,11... | collective-permute-start | bytes 270344 | tf_op jit(solution)/shard_map/ppermute | solution.py:477
  127.8 5.1 %collective-permute-start.12 = (f32[176,128]{1,0:T(8,128)S(1)}, f32[176,128]{1,0:T(8,128)S(1)}, u32[]{:S(2)}, u32[]{:S(2)}) collective-permute-start(f32[176,128]{1,0:T(8,128)S(1)} %pad_maximum_fusion.6), channel_id=1, source_target_pairs={{0,2},{1,3},{2,0},{3,1},{4,6},{5,7},{6,4},{7,5},{8,10},{9,11},{10,... | collective-permute-start | bytes 270344 | tf_op jit(solution)/shard_map/ppermute | solution.py:477
  130.2 4.6 %collective-permute-start.22 = (f32[176,128]{1,0:T(8,128)S(1)}, f32[176,128]{1,0:T(8,128)S(1)}, u32[]{:S(2)}, u32[]{:S(2)}) collective-permute-start(f32[176,128]{1,0:T(8,128)S(1)} %pad_maximum_fusion.7), channel_id=1, source_target_pairs={{0,16},{8,24},{16,0},{24,8},{1,17},{9,25},{17,1},{25,9},{2,18},{10... | collective-permute-start | bytes 270344 | tf_op jit(solution)/shard_map/ppermute | solution.py:477
  132.2 5.6 %collective-permute-start.33 = (f32[352,128]{1,0:T(8,128)S(1)}, f32[352,128]{1,0:T(8,128)S(1)}, u32[]{:S(2)}, u32[]{:S(2)}) collective-permute-start(f32[352,128]{1,0:T(8,128)S(1)} %pad_maximum_fusion.5), channel_id=1, source_target_pairs={{0,16},{8,24},{16,0},{24,8},{1,17},{9,25},{17,1},{25,9},{2,18},{10... | collective-permute-start | bytes 540680 | tf_op jit(solution)/shard_map/ppermute | solution.py:477
  132.9 5.6 %collective-permute-start.13 = (f32[352,128]{1,0:T(8,128)S(1)}, f32[352,128]{1,0:T(8,128)S(1)}, u32[]{:S(2)}, u32[]{:S(2)}) collective-permute-start(f32[352,128]{1,0:T(8,128)S(1)} %pad_maximum_fusion.3), channel_id=1, source_target_pairs={{0,1},{1,0},{2,3},{3,2},{4,5},{5,4},{6,7},{7,6},{8,9},{9,8},{10,11... | collective-permute-start | bytes 540680 | tf_op jit(solution)/shard_map/ppermute | solution.py:477
  134.8 6.5 %collective-permute-start.23 = (f32[352,128]{1,0:T(8,128)S(1)}, f32[352,128]{1,0:T(8,128)S(1)}, u32[]{:S(2)}, u32[]{:S(2)}) collective-permute-start(f32[352,128]{1,0:T(8,128)S(1)} %pad_maximum_fusion.4), channel_id=1, source_target_pairs={{0,2},{1,3},{2,0},{3,1},{4,6},{5,7},{6,4},{7,5},{8,10},{9,11},{10,... | collective-permute-start | bytes 540680 | tf_op jit(solution)/shard_map/ppermute | solution.py:477
  137.8 7.5 %collective-permute-start.34 = (f32[704,128]{1,0:T(8,128)S(1)}, f32[704,128]{1,0:T(8,128)S(1)}, u32[]{:S(2)}, u32[]{:S(2)}) collective-permute-start(f32[704,128]{1,0:T(8,128)S(1)} %pad_maximum_fusion.2.rest_8_), channel_id=1, source_target_pairs={{0,2},{1,3},{2,0},{3,1},{4,6},{5,7},{6,4},{7,5},{8,10},{9,11},{10,... | collective-permute-start | bytes 1081352 | tf_op jit(solution)/shard_map/ppermute | solution.py:477
  138.4 6.9 %collective-permute-start.35 = (f32[704,128]{1,0:T(8,128)S(1)}, f32[704,128]{1,0:T(8,128)S(1)}, u32[]{:S(2)}, u32[]{:S(2)}) collective-permute-start(f32[704,128]{1,0:T(8,128)S(1)} %pad_maximum_fusion.2.rest_8_), channel_id=1, source_target_pairs={{0,8},{8,0},{16,24},{24,16},{1,9},{9,1},{17,25},{25,17},{2,10},{10... | collective-permute-start | bytes 1081352 | tf_op jit(solution)/shard_map/ppermute | solution.py:477
  141.3 8.6 %collective-permute-start.14 = (f32[704,128]{1,0:T(8,128)S(1)}, f32[704,128]{1,0:T(8,128)S(1)}, u32[]{:S(2)}, u32[]{:S(2)}) collective-permute-start(f32[704,128]{1,0:T(8,128)S(1)} %pad_maximum_fusion.rest_0_), channel_id=1, source_target_pairs={{0,16},{8,24},{16,0},{24,8},{1,17},{9,25},{17,1},{25,9},{2,18},{10... | collective-permute-start | bytes 1081352 | tf_op jit(solution)/shard_map/ppermute | solution.py:477
  142.8 8.7 %collective-permute-start.24 = (f32[704,128]{1,0:T(8,128)S(1)}, f32[704,128]{1,0:T(8,128)S(1)}, u32[]{:S(2)}, u32[]{:S(2)}) collective-permute-start(f32[704,128]{1,0:T(8,128)S(1)} %pad_maximum_fusion.1.rest_4_), channel_id=1, source_target_pairs={{0,1},{1,0},{2,3},{3,2},{4,5},{5,4},{6,7},{7,6},{8,9},{9,8},{10,11... | collective-permute-start | bytes 1081352 | tf_op jit(solution)/shard_map/ppermute | solution.py:477
  143.4 8.3 %collective-permute-start.15 = (f32[704,128]{1,0:T(8,128)S(1)}, f32[704,128]{1,0:T(8,128)S(1)}, u32[]{:S(2)}, u32[]{:S(2)}) collective-permute-start(f32[704,128]{1,0:T(8,128)S(1)} %pad_maximum_fusion.rest_0_), channel_id=1, source_target_pairs={{0,8},{8,0},{16,24},{24,16},{1,9},{9,1},{17,25},{25,17},{2,10},{10... | collective-permute-start | bytes 1081352 | tf_op jit(solution)/shard_map/ppermute | solution.py:477
  145.3 6.5 %collective-permute-start.25 = (f32[704,128]{1,0:T(8,128)S(1)}, f32[704,128]{1,0:T(8,128)S(1)}, u32[]{:S(2)}, u32[]{:S(2)}) collective-permute-start(f32[704,128]{1,0:T(8,128)S(1)} %pad_maximum_fusion.1.rest_4_), channel_id=1, source_target_pairs={{0,8},{8,0},{16,24},{24,16},{1,9},{9,1},{17,25},{25,17},{2,10},{10... | collective-permute-start | bytes 1081352 | tf_op jit(solution)/shard_map/ppermute | solution.py:477
  145.3 6.5 %collective-permute-start.36 = (f32[704,128]{1,0:T(8,128)S(1)}, f32[704,128]{1,0:T(8,128)S(1)}, u32[]{:S(2)}, u32[]{:S(2)}) collective-permute-start(f32[704,128]{1,0:T(8,128)S(1)} %collective-permute-done.34.rest_9_), channel_id=1, source_target_pairs={{0,8},{8,0},{16,24},{24,16},{1,9},{9,1},{17,25},{25,17},{2,10},{10... | collective-permute-start | bytes 1081352 | tf_op jit(solution)/shard_map/ppermute | solution.py:477
  (31 other events, 253.9 us)

commit v3 on v2

--- a/solution.py
+++ b/solution.py
@@ -12,6 +12,7 @@
 TILE = 256
 LANES = 128
 COLORS = 3
+AHEAD = 4
 PARAMS = pltpu.CompilerParams(vmem_limit_bytes=60 * 1024 * 1024)
 ANY = pl.BlockSpec(memory_space=pl.ANY)
 VMEM = pl.BlockSpec(memory_space=pltpu.VMEM)
@@ -34,7 +35,7 @@
         t = t % (2 * self.tiles)
         for net in range(2):
             if t < self.tiles:
-                tile = self.first[net][:, t * TILE : (t + 1) * TILE]
+                tile = self.first[net][t]
             else:
                 t0 = (t - self.tiles) * TILE
                 tile = self.second[net][t0 : t0 + TILE, :]
@@ -64,13 +65,43 @@
                 pltpu.matmul_pop(self.accs[net][t])
 
 
-def step_copies(own, received, core, half, rows, steps, buffer, sems, k):
+def start_step(own, received, core, rows, steps, buffer, sems, k):
     local = lax.rem(k, steps)
-    from_own = pltpu.make_async_copy(
-        own.at[local, pl.ds(pl.multiple_of(core * rows, 8), rows), :], buffer.at[k], sems.at[k]
-    )
-    from_mate = pltpu.make_async_copy(received.at[local], buffer.at[k], sems.at[k])
-    return from_own, from_mate
+    mine = k // steps == core
+
+    @pl.when(mine)
+    def _():
+        source = own.at[local, pl.ds(pl.multiple_of(core * rows, 8), rows), :]
+        pltpu.make_async_copy(source, buffer.at[k], sems.at[k]).start()
+
+    @pl.when(jnp.logical_not(mine))
+    def _():
+        pltpu.make_async_copy(received.at[local], buffer.at[k], sems.at[k]).start()
+
+
+def store_step(source, kept, sent, core, rows, steps, sem, k):
+    local = lax.rem(k, steps)
+    mine = k // steps == core
+
+    @pl.when(mine)
+    def _():
+        target = kept.at[local, pl.ds(pl.multiple_of(core * rows, 8), rows), :]
+        pltpu.make_async_copy(source, target, sem).start()
+
+    @pl.when(jnp.logical_not(mine))
+    def _():
+        pltpu.make_async_copy(source, sent.at[local], sem).start()
+
+
+def weight_copies(first, second, first_buf, second_buf, sem):
+    copies = []
+    for net in range(2):
+        for j in range(first_buf.shape[1]):
+            tile = first[net].at[:, pl.ds(j * TILE, TILE)]
+            copies.append(pltpu.make_async_copy(tile, first_buf.at[net, j], sem))
+    for net in range(2):
+        copies.append(pltpu.make_async_copy(second[net], second_buf.at[net], sem))
+    return copies
 
 
 def forward_kernel(
@@ -95,44 +126,31 @@
     incoming, rest = (rest[0], rest[1:]) if turn > 0 else (None, rest)
     if full:
         final, states, states_send, q_out, u_out, v_out, a_out = rest[:7]
-        noise_buf, in_sems, out_sem, z_buf, q_buf, u_buf, v_buf, a_buf = rest[7:]
+        noise_buf, in_sems, weight_sem, first_buf, second_buf = rest[7:12]
+        out_sem, z_buf, q_buf, u_buf, v_buf, a_buf = rest[12:]
     else:
-        final, noise_buf, in_sems = rest
+        final, noise_buf, in_sems, weight_sem, first_buf, second_buf = rest
     window = 2 * steps
     core = info[0]
     stage = info[1]
     hidden = drift_inner.shape[1]
-
-    def start(k, carry):
-        mine = k // steps == core
-        from_own, from_mate = step_copies(
-            own_noise, mate_noise, core, None, rows, steps, noise_buf, in_sems, k
-        )
-
-        @pl.when(mine)
-        def _():
-            from_own.start()
-
-        @pl.when(jnp.logical_not(mine))
-        def _():
-            from_mate.start()
-
-        return carry
-
-    def state_copies(k):
-        local = lax.rem(k, steps)
-        keep = pltpu.make_async_copy(
-            z_buf.at[k],
-            states.at[local, pl.ds(pl.multiple_of(core * rows, 8), rows), :],
-            out_sem,
-        )
-        send = pltpu.make_async_copy(z_buf.at[k], states_send.at[local], out_sem)
-        return keep, send
+    weights = weight_copies(
+        (drift_inner, noise_inner), (drift_outer, noise_outer), first_buf, second_buf, weight_sem
+    )
+    if incoming is None:
+        begin = initial.at[pl.ds(pl.multiple_of(core * rows, 8), rows), :]
+        weights.append(pltpu.make_async_copy(begin, final, weight_sem))
+
+    def fetch(k):
+        start_step(own_noise, mate_noise, core, rows, steps, noise_buf, in_sems, k)
 
     def saved_copies(k):
         return [
             pltpu.make_async_copy(buf.at[k], out.at[k], out_sem)
-            for buf, out in ((q_buf, q_out), (u_buf, u_out), (v_buf, v_out), (a_buf, a_out))
+            for buf, out in ((q_buf, q_out), (a_buf, a_out))
+        ] + [
+            pltpu.make_async_copy(buf.at[:, k], out.at[:, k], out_sem)
+            for buf, out in ((u_buf, u_out), (v_buf, v_out))
         ]
 
     def body(pipe, k, carry):
@@ -148,8 +166,12 @@
             bias = (drift_hidden, noise_hidden)[net]
             value = jnp.tanh(raw + bias[:, cols]).astype(jnp.bfloat16)
             if full:
-                saved[net][k, :, cols] = value
+                saved[net][j, k] = value
             return value
+
+        @pl.when(k + AHEAD < window)
+        def _():
+            fetch(k + AHEAD)
 
         drift, spread = pipe.run((q, q), act)
         drift = drift + drift_offset[...]
@@ -161,28 +183,24 @@
         if full:
             a_buf[k] = noise * s * (1.0 - s)
             z_buf[k] = following
-            mine = k // steps == core
-            keep, send = state_copies(k)
-
-            @pl.when(mine)
-            def _():
-                keep.start()
-
-            @pl.when(jnp.logical_not(mine))
-            def _():
-                send.start()
-
+            store_step(z_buf.at[k], states, states_send, core, rows, steps, out_sem, k)
             for copy in saved_copies(k):
                 copy.start()
         return carry
 
     def solve(*accs):
-        lax.fori_loop(0, window, start, 0)
-        begin = initial[pl.ds(pl.multiple_of(core * rows, 8), rows), :]
+        for copy in weights:
+            copy.start()
+        for k in range(AHEAD):
+            fetch(k)
+        for copy in weights:
+            copy.wait()
         if incoming is not None:
-            begin = jnp.where(stage == 0, begin, incoming[...])
-        final[...] = begin
-        pipe = Pipe((drift_inner, noise_inner), (drift_outer, noise_outer), accs)
+            begin = initial[pl.ds(pl.multiple_of(core * rows, 8), rows), :]
+            final[...] = jnp.where(stage == 0, begin, incoming[...])
+        pipe = Pipe(
+            [first_buf.at[net] for net in range(2)], [second_buf.at[net] for net in range(2)], accs
+        )
         pipe.prime()
         lax.fori_loop(0, window, functools.partial(body, pipe), 0)
         pipe.drain(jnp.zeros((rows, TILE), jnp.bfloat16))
@@ -194,7 +212,7 @@
     if full:
 
         def finish(k, carry):
-            state_copies(k)[1].wait()
+            pltpu.make_async_copy(z_buf.at[k], states_send.at[0], out_sem).wait()
             for copy in saved_copies(k):
                 copy.wait()
             return carry
@@ -226,50 +244,36 @@
     incoming, rest = (rest[0], rest[1:]) if turn > 0 else (None, rest)
     if full:
         final, adjoints, adjoints_send, keep_out, send_out = rest[:5]
-        (c_buf, u_buf, v_buf, a_buf, in_sems, q_sem, out_sem, q_buf) = rest[5:13]
-        (e_buf, pb_buf, rb_buf, fb_buf, gb_buf, qt_buf) = rest[13:19]
-        (p_sum, r_sum, f_sum, g_sum, packed) = rest[19:]
+        rest = rest[5:]
     else:
-        final, c_buf, u_buf, v_buf, a_buf, in_sems = rest
+        final, rest = rest[0], rest[1:]
+    c_buf, u_buf, v_buf, a_buf, in_sems, weight_sem, first_buf, second_buf = rest[:8]
+    if full:
+        (out_sem, q_buf, e_buf, pb_buf, rb_buf, fb_buf, gb_buf, qt_buf) = rest[8:16]
+        (p_sum, r_sum, f_sum, g_sum, packed) = rest[16:]
     window = 2 * steps
     core = info[0]
     stage = info[1]
     width, hidden = drift_outer_t.shape
+    weights = weight_copies(
+        (drift_outer_t, noise_outer_t),
+        (drift_inner_t, noise_inner_t),
+        first_buf,
+        second_buf,
+        weight_sem,
+    )
 
     def saved_copies(k):
-        return [
-            pltpu.make_async_copy(src.at[k], buf.at[k], in_sems.at[k])
-            for src, buf in ((u_in, u_buf), (v_in, v_buf), (a_in, a_buf))
+        whole = ((a_in, a_buf), (q_in, q_buf)) if full else ((a_in, a_buf),)
+        return [pltpu.make_async_copy(src.at[k], buf.at[k], in_sems.at[k]) for src, buf in whole] + [
+            pltpu.make_async_copy(src.at[:, k], buf.at[:, k], in_sems.at[k])
+            for src, buf in ((u_in, u_buf), (v_in, v_buf))
         ]
 
-    def start(n, carry):
-        k = window - 1 - n
-        mine = k // steps == core
-        from_own, from_mate = step_copies(
-            own_cotangent, mate_cotangent, core, None, rows, steps, c_buf, in_sems, k
-        )
-
-        @pl.when(mine)
-        def _():
-            from_own.start()
-
-        @pl.when(jnp.logical_not(mine))
-        def _():
-            from_mate.start()
-
+    def fetch(k):
+        start_step(own_cotangent, mate_cotangent, core, rows, steps, c_buf, in_sems, k)
         for copy in saved_copies(k):
             copy.start()
-        return carry
-
-    def adjoint_copies(k):
-        local = lax.rem(k, steps)
-        keep = pltpu.make_async_copy(
-            e_buf.at[k],
-            adjoints.at[local, pl.ds(pl.multiple_of(core * rows, 8), rows), :],
-            out_sem,
-        )
-        send = pltpu.make_async_copy(e_buf.at[k], adjoints_send.at[local], out_sem)
-        return keep, send
 
     def partial(x):
         return jnp.sum(x.reshape(rows // 8, 8, x.shape[1]), 0)
@@ -286,53 +290,55 @@
         fb = f.astype(jnp.bfloat16)
         gb = g.astype(jnp.bfloat16)
         if full:
-            fb_buf[:, pl.ds(pl.multiple_of(k * rows, rows), rows)] = fb.T
-            gb_buf[:, pl.ds(pl.multiple_of(k * rows, rows), rows)] = gb.T
-            qt_buf[:, pl.ds(pl.multiple_of(k * rows, rows), rows)] = q_buf[k].T
+            part = k // per_tile
+            lanes = pl.ds(pl.multiple_of(lax.rem(k, per_tile) * rows, rows), rows)
+            fb_buf[part, :, lanes] = fb.T
+            gb_buf[part, :, lanes] = gb.T
+            qt_buf[part, :, lanes] = q_buf[k].T
             f_sum[...] += partial(f)
             g_sum[...] += partial(g)
 
         def act(net, j, raw):
             cols = slice(j * TILE, (j + 1) * TILE)
-            value = (u_buf, v_buf)[net][k, :, cols].astype(jnp.float32)
+            value = (u_buf, v_buf)[net][j, k].astype(jnp.float32)
             back = raw * (1.0 - value * value)
             low = back.astype(jnp.bfloat16)
             if full:
                 (p_sum, r_sum)[net][:, cols] += partial(back)
-                (pb_buf, rb_buf)[net][k, :, cols] = low
+                (pb_buf, rb_buf)[net][j, k] = low
             return low
+
+        @pl.when(k >= AHEAD)
+        def _():
+            fetch(k - AHEAD)
 
         drift_part, noise_part = pipe.run((fb, gb), act)
         result = final[...] + (drift_part + noise_part)
         final[...] = result
         if full:
             e_buf[k] = result
-            mine = k // steps == core
-            keep, send = adjoint_copies(k)
-
-            @pl.when(mine)
-            def _():
-                keep.start()
-
-            @pl.when(jnp.logical_not(mine))
-            def _():
-                send.start()
-
+            store_step(e_buf.at[k], adjoints, adjoints_send, core, rows, steps, out_sem, k)
         return carry
 
+    per_tile = TILE // rows
+
     def solve(*accs):
-        lax.fori_loop(0, window, start, 0)
+        for copy in weights:
+            copy.start()
+        for n in range(AHEAD):
+            fetch(window - 1 - n)
         if full:
-            q_copy = pltpu.make_async_copy(q_in, q_buf, q_sem)
-            q_copy.start()
             for ref in (p_sum, r_sum, f_sum, g_sum):
                 ref[...] = jnp.zeros_like(ref)
-            q_copy.wait()
         begin = jnp.zeros(final.shape, jnp.float32)
         if incoming is not None:
             begin = jnp.where(stage == stages - 1, begin, incoming[...])
         final[...] = begin
-        pipe = Pipe((drift_outer_t, noise_outer_t), (drift_inner_t, noise_inner_t), accs)
+        for copy in weights:
+            copy.wait()
+        pipe = Pipe(
+            [first_buf.at[net] for net in range(2)], [second_buf.at[net] for net in range(2)], accs
+        )
         pipe.prime()
         lax.fori_loop(0, window, functools.partial(body, pipe), 0)
         pipe.drain(jnp.zeros((rows, TILE), jnp.bfloat16))
@@ -349,7 +355,6 @@
     rights = ((pb_buf, u_buf), (rb_buf, v_buf))
 
     def products(*accs):
-        per_step = TILE // rows
         chain = [
             (j, which, c)
             for j in range(hidden // TILE)
@@ -360,9 +365,7 @@
         def push(n):
             j, which, c = chain[n]
             for net in range(2):
-                block = rights[net][which][
-                    c * per_step : (c + 1) * per_step, :, j * TILE : (j + 1) * TILE
-                ]
+                block = rights[net][which][j, c * per_tile : (c + 1) * per_tile]
                 pltpu.matmul_push_rhs(
                     block.reshape(TILE, TILE), staging_register=n % 2, mxu_index=net
                 )
@@ -372,7 +375,7 @@
         for n, (j, which, c) in enumerate(chain):
             slot = (2 * j + which) % 4
             for net in range(2):
-                left = lefts[net][which][:, c * TILE : (c + 1) * TILE]
+                left = lefts[net][which][c]
                 pltpu.matmul_acc_lhs(accs[4 * net + slot], left, load_staged_rhs=n % 2)
             if n + 2 < len(chain):
                 push(n + 2)
@@ -382,8 +385,9 @@
                     for i in range(TILE // LANES):
                         row = which * per_matrix + (j * (TILE // LANES) + i) * width
                         packed[net, row : row + width, :] = grad[:, i * LANES : (i + 1) * LANES]
-
-    pl.run_scoped(products, *accumulators(width, 4))
+                        done[row // width] = True
+                release()
+
     for net, (hidden_sum, offset_sum) in enumerate(((p_sum, f_sum), (r_sum, g_sum))):
         base = 2 * per_matrix
         hidden_total = jnp.sum(hidden_sum[...], 0, keepdims=True)
@@ -395,32 +399,41 @@
         for i in range(width // LANES):
             packed[net, base + i : base + i + 1, :] = offset_total[:, i * LANES : (i + 1) * LANES]
 
-    def grad_copies(out, net):
-        copies = []
-        for color in range(COLORS):
-            me = info[2 + color]
-            for s in range(blocks):
-                source = (color * blocks + s) * block_rows
-                place = color * blocks + ((s ^ (blocks - 1)) ^ me)
-                copies.append(
-                    pltpu.make_async_copy(
-                        packed.at[net, pl.ds(source, block_rows), :],
-                        out.at[pl.ds(pl.multiple_of(place * block_rows, 8), block_rows), :],
-                        out_sem,
-                    )
-                )
-        return copies
-
-    for copy in grad_copies(send_out, 1 - core) + grad_copies(keep_out, core):
-        copy.start()
+    every_block = [(color, b) for color in range(COLORS) for b in range(blocks)]
+
+    def grad_copies(color, b):
+        source = (color * blocks + b) * block_rows
+        place = color * blocks + ((b ^ (blocks - 1)) ^ info[2 + color])
+        target = pl.ds(pl.multiple_of(place * block_rows, 8), block_rows)
+        return [
+            pltpu.make_async_copy(
+                packed.at[net, pl.ds(source, block_rows), :], out.at[target, :], out_sem
+            )
+            for out, net in ((send_out, 1 - core), (keep_out, core))
+        ]
+
+    waiting = list(every_block)
+    done = [False] * (2 * per_matrix // width)
+
+    def release():
+        for color, b in list(waiting):
+            begin = (color * blocks + b) * block_rows
+            end = min(begin + block_rows, 2 * per_matrix)
+            if all(done[row // width] for row in range(begin, end)):
+                waiting.remove((color, b))
+                for copy in grad_copies(color, b):
+                    copy.start()
+
+    pl.run_scoped(products, *accumulators(width, 4))
 
     def finish(k, carry):
-        adjoint_copies(k)[1].wait()
+        pltpu.make_async_copy(e_buf.at[k], adjoints_send.at[0], out_sem).wait()
         return carry
 
     lax.fori_loop(0, window, finish, 0)
-    for copy in grad_copies(send_out, 1 - core) + grad_copies(keep_out, core):
-        copy.wait()
+    for color, b in every_block:
+        for copy in grad_copies(color, b):
+            copy.wait()
 
 
 def finish_kernel(blocks, block_rows, width, hidden, limit, info, *rest):
@@ -549,6 +562,13 @@
     )
     turned = (drift_inner.T, drift_outer.T, noise_inner.T, noise_outer.T)
 
+    tiles = hidden // TILE
+    weight_scratch = (
+        pltpu.SemaphoreType.DMA,
+        pltpu.VMEM((2, tiles, width, TILE), bf16),
+        pltpu.VMEM((2, hidden, width), bf16),
+    )
+
     def sds(shape, dtype=f32):
         return jax.ShapeDtypeStruct(shape, dtype)
 
@@ -558,14 +578,15 @@
         scratch = [
             pltpu.VMEM((window, rows, width), f32),
             pltpu.SemaphoreType.DMA((window,)),
+            *weight_scratch,
         ]
         if full:
             out_shape += [
                 sds((steps, local_rows, width)),
                 sds((steps, rows, width)),
                 sds((window, rows, width), bf16),
-                sds((window, rows, hidden), bf16),
-                sds((window, rows, hidden), bf16),
+                sds((tiles, window, rows, TILE), bf16),
+                sds((tiles, window, rows, TILE), bf16),
                 sds((window, rows, width)),
             ]
             out_specs += [ANY] * 6
@@ -573,14 +594,16 @@
                 pltpu.SemaphoreType.DMA,
                 pltpu.VMEM((window, rows, width), f32),
                 pltpu.VMEM((window, rows, width), bf16),
-                pltpu.VMEM((window, rows, hidden), bf16),
-                pltpu.VMEM((window, rows, hidden), bf16),
+                pltpu.VMEM((tiles, window, rows, TILE), bf16),
+                pltpu.VMEM((tiles, window, rows, TILE), bf16),
                 pltpu.VMEM((window, rows, width), f32),
             ]
         return pl.pallas_call(
             functools.partial(forward_kernel, turn, full, steps, rows),
             out_shape=out_shape,
-            in_specs=[SMEM, VMEM, ANY, ANY] + [VMEM] * (8 + (turn > 0)),
+            in_specs=[SMEM, ANY if turn == 0 else VMEM, ANY, ANY]
+            + [ANY, VMEM] * 4
+            + [VMEM] * (turn > 0),
             out_specs=out_specs,
             scratch_shapes=scratch,
             compiler_params=PARAMS,
@@ -604,10 +627,11 @@
         out_specs = [VMEM]
         scratch = [
             pltpu.VMEM((window, rows, width), f32),
-            pltpu.VMEM((window, rows, hidden), bf16),
-            pltpu.VMEM((window, rows, hidden), bf16),
+            pltpu.VMEM((tiles, window, rows, TILE), bf16),
+            pltpu.VMEM((tiles, window, rows, TILE), bf16),
             pltpu.VMEM((window, rows, width), f32),
             pltpu.SemaphoreType.DMA((window,)),
+            *weight_scratch,
         ]
         if full:
             out_shape += [
@@ -619,14 +643,13 @@
             out_specs += [ANY] * 4
             scratch += [
                 pltpu.SemaphoreType.DMA,
-                pltpu.SemaphoreType.DMA,
                 pltpu.VMEM((window, rows, width), bf16),
                 pltpu.VMEM((window, rows, width), f32),
-                pltpu.VMEM((window, rows, hidden), bf16),
-                pltpu.VMEM((window, rows, hidden), bf16),
-                pltpu.VMEM((width, window * rows), bf16),
-                pltpu.VMEM((width, window * rows), bf16),
-                pltpu.VMEM((width, window * rows), bf16),
+                pltpu.VMEM((tiles, window, rows, TILE), bf16),
+                pltpu.VMEM((tiles, window, rows, TILE), bf16),
+                pltpu.VMEM((window * rows // TILE, width, TILE), bf16),
+                pltpu.VMEM((window * rows // TILE, width, TILE), bf16),
+                pltpu.VMEM((window * rows // TILE, width, TILE), bf16),
                 pltpu.VMEM((8, hidden), f32),
                 pltpu.VMEM((8, hidden), f32),
                 pltpu.VMEM((8, width), f32),
@@ -638,7 +661,7 @@
                 backward_kernel, turn, stages, full, steps, rows, blocks, block_rows
             ),
             out_shape=out_shape,
-            in_specs=[SMEM] + [ANY] * 6 + [VMEM] * (4 + (turn > 0)),
+            in_specs=[SMEM] + [ANY] * 10 + [VMEM] * (turn > 0),
             out_specs=out_specs,
             scratch_shapes=scratch,
             compiler_params=PARAMS,

time: 161 us -> 156 us (0.969)
  Pallas kernels: 53.3 us -> 47.8 us
    pallas_call x2, Pallas kernels: 25.6 us -> 19.3 us  [backward(): pl.pallas_call(functools.partial(backward_kernel, turn, stages, full, ste...]
  transfers between devices with their start and end apart: 37 -> 37, of which waited for: 20 -> 20; matrix products, arithmetic and copies ran while one was open for 4% -> 4% of each run, Pallas kernels for 14% -> 15%
where the time goes in v3:
time: 156 us; the launch traced here: 155 us
  waiting for transfers between devices  56.1 us (36%)
  Pallas kernels  47.8 us (31%)
  starting transfers between devices  35.4 us (23%)
  local copies, waits for them, and re-layouts  13.2 us (8%)
  other arithmetic  1.8 us (1%)
    ppermute x35, waiting for transfers between devices, flipped(): lax.ppermute(block, axis, [(i, i ^ bit) for i in range(lax.axis_size(axis...  40.1 us
    ppermute x35, starting transfers between devices, flipped(): lax.ppermute(block, axis, [(i, i ^ bit) for i in range(lax.axis_size(axis...  32.7 us
    pallas_call x2, Pallas kernels, forward(): pl.pallas_call(functools.partial(forward_kernel, turn, full, steps, rows)...  22.7 us
    pallas_call x2, Pallas kernels, backward(): pl.pallas_call(functools.partial(backward_kernel, turn, stages, full, ste...  19.3 us
    ppermute x2, waiting for transfers between devices, moved(): lax.ppermute(block, 'tm', [(i, i + distance) for i in range(count) if 0 <...  16 us
    unnamed x56, local copies, waits for them, and re-layouts  8.92 us
    pallas_call x1, Pallas kernels, shards(): pl.pallas_call(functools.partial(finish_kernel, blocks, block_rows, width...  5.79 us
    dynamic_slice x2, local copies, waits for them, and re-layouts, other_half(): return lax.dynamic_slice_in_dim(array, (1 - core) * rows, rows, 1)  3.5 us
  transfers between devices with their start and end apart: 37, of which 20 were waited for; matrix products, arithmetic and copies ran while one was open for 4% of the time, Pallas kernels for 15%

profile of v3, /device:TPU:0, one launch (start us, length us, event | category | flops | bytes accessed | tf_op | source)
XLA Modules:
  0.0 155.4 jit_solution(3939450313006351817)
XLA Ops:
  0.7 2.4 %constant_dynamic-slice_fusion.1 = f32[8,128,256]{2,1,0:T(8,128)} fusion(f32[8,256,256]{2,1,0:T(8,128)} %own_noise.3, s32[]{:T(128)S(6)} %select_n.73), kind=kLoop, calls=%fused_computation.57 | loop fusion | bytes 2097156 | tf_op jit(solution)/shard_map/dynamic_slice | solution.py:549
  6.2 10.8 %forward_light.1 = f32[128,256]{1,0:T(8,128)} custom-call(s32[5]{0:T(128)} %stack.23.info, f32[256,256]{1,0:T(8,128)} %initial.3, f32[8,256,256]{2,1,0:T(8,128)} %own_noise.3, f32[8,128,256]{2,1,0:T(8,128)} %collective-permute-done.mate_noise, bf16[256,1024]{1,0:T(8,128)(2,1)} %drift_inner.3, f32[1,1024]{1,0:T(1,128)} %bitcast.25, ...), custom_call_target="tpu_custom_call" | custom-call | tf_op jit(solution)/shard_map/forward_light/pallas_call | solution.py:601
  17.0 1.4 collective-permute-start.1
  23.2 11.9 %forward_full.1 = (f32[128,256]{1,0:T(8,128)}, f32[8,256,256]{2,1,0:T(8,128)}, f32[8,128,256]{2,1,0:T(8,128)}, bf16[16,128,256]{2,1,0:T(8,128)(2,1)}, bf16[4,16,...) custom-call(s32[5]{0:T(128)} %stack.23.info, f32[256,256]{1,0:T(8,128)} %initial.3, ...), custom_call_target="tpu_custom_call" | custom-call | tf_op jit(solution)/shard_map/forward_full/pallas_call | solution.py:601
  36.1 1.5 backward_light.1
  38.9 16.0 %collective-permute-done.4.rest_0_ = f32[128,256]{1,0:T(8,128)S(1)} collective-permute-done((f32[128,256]{1,0:T(8,128)}, f32[128,256]{1,0:T(8,128)S(1)}, u32[]{:S(2)}, u32[]{:S(2)}) %collective-permute-start.4) | collective-permute-done | bytes 131104 | tf_op jit(solution)/shard_map/ppermute | solution.py:495
  55.6 17.9 %backward_full.1 = (f32[128,256]{1,0:T(8,128)}, f32[8,256,256]{2,1,0:T(8,128)}, f32[8,128,256]{2,1,0:T(8,128)}, f32[4224,128]{1,0:T(8,128)}, f32[4224,128]{1,0:T(8,128)}) custom-call(s32[5]{0:T(128)} %stack.23.info, f32[8,256,256]{2,1,0:T(8,128)} %own_cotangent.3, f32[8,128,256]{2,1,0:T(8,128)} %copy-done.5, bf16[16,128,256]{2,1,0:T(8,128)(2,1)} %get-tuple-element.30.q_in, ...), custom_call_target="tpu_custom_call" | custom-call | tf_op jit(solution)/shard_map/backward_full/pallas_call | solution.py:659
  73.5 4.5 %collective-permute-done.6 = f32[4224,128]{1,0:T(8,128)S(1)} collective-permute-done((f32[4224,128]{1,0:T(8,128)}, f32[4224,128]{1,0:T(8,128)S(1)}, u32[]{:S(2)}, u32[]{:S(2)}) %collective-permute-start.6) | collective-permute-done | bytes 2162720 | tf_op jit(solution)/shard_map/ppermute | solution.py:490
  78.0 1.3 slice_add_fusion
  79.3 2.5 %collective-permute-start.27 = (f32[704,128]{1,0:T(8,128)S(1)}, f32[704,128]{1,0:T(8,128)S(1)}, u32[]{:S(2)}, u32[]{:S(2)}) collective-permute-start(f32[704,128]{1,0:T(8,128)S(1)} %get-tuple-element.55), channel_id=1, source_target_pairs={{0,2},{1,3},{2,0},{3,1},{4,6},{5,7},{6,4},{7,5},{8,10},{9,11},{10,... | collective-permute-start | bytes 1081352 | tf_op jit(solution)/shard_map/ppermute | solution.py:490
  81.8 1.6 %collective-permute-start.17 = (f32[704,128]{1,0:T(8,128)S(1)}, f32[704,128]{1,0:T(8,128)S(1)}, u32[]{:S(2)}, u32[]{:S(2)}) collective-permute-start(f32[704,128]{1,0:T(8,128)S(1)} %get-tuple-element.56), channel_id=1, source_target_pairs={{0,1},{1,0},{2,3},{3,2},{4,5},{5,4},{6,7},{7,6},{8,9},{9,8},{10,11... | collective-permute-start | bytes 1081352 | tf_op jit(solution)/shard_map/ppermute | solution.py:490
  83.4 7.1 %collective-permute-done.27 = f32[704,128]{1,0:T(8,128)S(1)} collective-permute-done((f32[704,128]{1,0:T(8,128)S(1)}, f32[704,128]{1,0:T(8,128)S(1)}, u32[]{:S(2)}, u32[]{:S(2)}) %collective-permute-start.27) | collective-permute-done | bytes 360480 | tf_op jit(solution)/shard_map/ppermute | solution.py:490
  90.6 1.5 collective-permute-done.17
  94.6 4.4 %collective-permute-done.28 = f32[352,128]{1,0:T(8,128)S(1)} collective-permute-done((f32[352,128]{1,0:T(8,128)S(1)}, f32[352,128]{1,0:T(8,128)S(1)}, u32[]{:S(2)}, u32[]{:S(2)}) %collective-permute-start.28) | collective-permute-done | bytes 180256 | tf_op jit(solution)/shard_map/ppermute | solution.py:490
  100.2 1.7 %collective-permute-start.19 = (f32[176,128]{1,0:T(8,128)S(1)}, f32[176,128]{1,0:T(8,128)S(1)}, u32[]{:S(2)}, u32[]{:S(2)}) collective-permute-start(f32[176,128]{1,0:T(8,128)S(1)} %get-tuple-element.50), channel_id=1, source_target_pairs={{0,16},{8,24},{16,0},{24,8},{1,17},{9,25},{17,1},{25,9},{2,18},{10... | collective-permute-start | bytes 270344 | tf_op jit(solution)/shard_map/ppermute | solution.py:490
  102.0 1.7 %collective-permute-start.9 = (f32[176,128]{1,0:T(8,128)S(1)}, f32[176,128]{1,0:T(8,128)S(1)}, u32[]{:S(2)}, u32[]{:S(2)}) collective-permute-start(f32[176,128]{1,0:T(8,128)S(1)} %get-tuple-element.51), channel_id=1, source_target_pairs={{0,2},{1,3},{2,0},{3,1},{4,6},{5,7},{6,4},{7,5},{8,10},{9,11},{10,... | collective-permute-start | bytes 270344 | tf_op jit(solution)/shard_map/ppermute | solution.py:490
  104.4 2.6 %collective-permute-start.30 = (f32[88,128]{1,0:T(8,128)S(1)}, f32[88,128]{1,0:T(8,128)S(1)}, u32[]{:S(2)}, u32[]{:S(2)}) collective-permute-start(f32[88,128]{1,0:T(8,128)S(1)} %slice_add_fusion.18), channel_id=1, source_target_pairs={{0,4},{1,5},{2,6},{3,7},{4,0},{5,1},{6,2},{7,3},{8,12},{9,13},{10,... | collective-permute-start | bytes 135176 | tf_op jit(solution)/shard_map/ppermute | solution.py:490
  107.0 2.4 %collective-permute-done.30 = f32[88,128]{1,0:T(8,128)S(1)} collective-permute-done((f32[88,128]{1,0:T(8,128)S(1)}, f32[88,128]{1,0:T(8,128)S(1)}, u32[]{:S(2)}, u32[]{:S(2)}) %collective-permute-start.30) | collective-permute-done | bytes 45088 | tf_op jit(solution)/shard_map/ppermute | solution.py:490
  109.5 3.1 %collective-permute-start.20 = (f32[88,128]{1,0:T(8,128)S(1)}, f32[88,128]{1,0:T(8,128)S(1)}, u32[]{:S(2)}, u32[]{:S(2)}) collective-permute-start(f32[88,128]{1,0:T(8,128)S(1)} %get-tuple-element.47), channel_id=1, source_target_pairs={{0,4},{1,5},{2,6},{3,7},{4,0},{5,1},{6,2},{7,3},{8,12},{9,13},{10,... | collective-permute-start | bytes 135176 | tf_op jit(solution)/shard_map/ppermute | solution.py:490
  113.2 2.8 %collective-permute-start.31 = (f32[88,128]{1,0:T(8,128)S(1)}, f32[88,128]{1,0:T(8,128)S(1)}, u32[]{:S(2)}, u32[]{:S(2)}) collective-permute-start(f32[88,128]{1,0:T(8,128)S(1)} %get-tuple-element.46), channel_id=1, source_target_pairs={{0,4},{1,5},{2,6},{3,7},{4,0},{5,1},{6,2},{7,3},{8,12},{9,13},{10,... | collective-permute-start | bytes 135176 | tf_op jit(solution)/shard_map/ppermute | solution.py:490
  116.0 1.9 %collective-permute-done.10 = f32[88,128]{1,0:T(8,128)S(1)} collective-permute-done((f32[88,128]{1,0:T(8,128)S(1)}, f32[88,128]{1,0:T(8,128)S(1)}, u32[]{:S(2)}, u32[]{:S(2)}) %collective-permute-start.10) | collective-permute-done | bytes 45088 | tf_op jit(solution)/shard_map/ppermute | solution.py:490
  118.1 2.8 %collective-permute-start.21 = (f32[88,128]{1,0:T(8,128)S(1)}, f32[88,128]{1,0:T(8,128)S(1)}, u32[]{:S(2)}, u32[]{:S(2)}) collective-permute-start(f32[88,128]{1,0:T(8,128)S(1)} %get-tuple-element.58), channel_id=1, source_target_pairs={{0,4},{1,5},{2,6},{3,7},{4,0},{5,1},{6,2},{7,3},{8,12},{9,13},{10,... | collective-permute-start | bytes 135176 | tf_op jit(solution)/shard_map/ppermute | solution.py:490
  123.0 2.4 %collective-permute-start.12 = (f32[176,128]{1,0:T(8,128)S(1)}, f32[176,128]{1,0:T(8,128)S(1)}, u32[]{:S(2)}, u32[]{:S(2)}) collective-permute-start(f32[176,128]{1,0:T(8,128)S(1)} %pad_maximum_fusion.6), channel_id=1, source_target_pairs={{0,2},{1,3},{2,0},{3,1},{4,6},{5,7},{6,4},{7,5},{8,10},{9,11},{10,... | collective-permute-start | bytes 270344 | tf_op jit(solution)/shard_map/ppermute | solution.py:490
  125.4 2.0 %collective-permute-start.22 = (f32[176,128]{1,0:T(8,128)S(1)}, f32[176,128]{1,0:T(8,128)S(1)}, u32[]{:S(2)}, u32[]{:S(2)}) collective-permute-start(f32[176,128]{1,0:T(8,128)S(1)} %pad_maximum_fusion.7), channel_id=1, source_target_pairs={{0,16},{8,24},{16,0},{24,8},{1,17},{9,25},{17,1},{25,9},{2,18},{10... | collective-permute-start | bytes 270344 | tf_op jit(solution)/shard_map/ppermute | solution.py:490
  130.1 1.3 collective-permute-start.23
  131.4 1.6 %collective-permute-done.33 = f32[352,128]{1,0:T(8,128)S(1)} collective-permute-done((f32[352,128]{1,0:T(8,128)S(1)}, f32[352,128]{1,0:T(8,128)S(1)}, u32[]{:S(2)}, u32[]{:S(2)}) %collective-permute-start.33) | collective-permute-done | bytes 180256 | tf_op jit(solution)/shard_map/ppermute | solution.py:490
  133.7 2.9 %collective-permute-done.23 = f32[352,128]{1,0:T(8,128)S(1)} collective-permute-done((f32[352,128]{1,0:T(8,128)S(1)}, f32[352,128]{1,0:T(8,128)S(1)}, u32[]{:S(2)}, u32[]{:S(2)}) %collective-permute-start.23) | collective-permute-done | bytes 180256 | tf_op jit(solution)/shard_map/ppermute | solution.py:490
  136.5 1.4 collective-permute-start.14
  138.6 1.9 %collective-permute-done.34.rest_9_ = f32[704,128]{1,0:T(8,128)S(1)} collective-permute-done((f32[704,128]{1,0:T(8,128)S(1)}, f32[704,128]{1,0:T(8,128)S(1)}, u32[]{:S(2)}, u32[]{:S(2)}) %collective-permute-start.34) | collective-permute-done | bytes 360480 | tf_op jit(solution)/shard_map/ppermute | solution.py:490
  141.1 4.1 %collective-permute-done.14.rest_1_ = f32[704,128]{1,0:T(8,128)S(1)} collective-permute-done((f32[704,128]{1,0:T(8,128)S(1)}, f32[704,128]{1,0:T(8,128)S(1)}, u32[]{:S(2)}, u32[]{:S(2)}) %collective-permute-start.14) | collective-permute-done | bytes 360480 | tf_op jit(solution)/shard_map/ppermute | solution.py:490
  145.1 1.6 %collective-permute-done.24.rest_5_ = f32[704,128]{1,0:T(8,128)S(1)} collective-permute-done((f32[704,128]{1,0:T(8,128)S(1)}, f32[704,128]{1,0:T(8,128)S(1)}, u32[]{:S(2)}, u32[]{:S(2)}) %collective-permute-start.24) | collective-permute-done | bytes 360480 | tf_op jit(solution)/shard_map/ppermute | solution.py:490
  149.6 5.8 %finish.1 = (f32[256,1024]{1,0:T(8,128)}, f32[1,1024]{1,0:T(1,128)}, f32[1024,256]{1,0:T(8,128)}, f32[1,256]{1,0:T(1,128)}, f32[256,1024]{1,0:T(8,128)}, /*index...) custom-call(s32[5]{0:T(128)} %stack.23.info, f32[704,128]{1,0:T(8,128)} %copy-done.8, f32[704,128]{1,0:T(8,128)} %copy-done.12, ...), custom_call_target="tpu_custom_call" | custom-call | tf_op jit(solution)/shard_map/finish/pallas_call | solution.py:705
  (123 shorter events, 25.5 us)
Async XLA Ops:
  4.7 30.4 %collective-permute-start.3 = (f32[8,128,256]{2,1,0:T(8,128)}, f32[8,128,256]{2,1,0:T(8,128)S(1)}, u32[]{:S(2)}, u32[]{:S(2)}) collective-permute-start(f32[8,128,256]{2,1,0:T(8,128)} %constant_dynamic-slice_fusion), channel_id=1, source_target_pairs={{0,8},{8,0},{16,24},{24,16},{1,9},{9,1},{17,25},{25,17},{2,10},{10... | collective-permute-start | bytes 3145736 | tf_op jit(solution)/shard_map/ppermute | solution.py:490
  17.0 5.5 %collective-permute-start.1 = (f32[128,256]{1,0:T(8,128)}, f32[128,256]{1,0:T(8,128)S(1)}, u32[]{:S(2)}, u32[]{:S(2)}) collective-permute-start(f32[128,256]{1,0:T(8,128)} %forward_light.1), channel_id=1, source_target_pairs={{0,16},{8,24},{1,17},{9,25},{2,18},{10,26},{3,19},{11,27},{4,20},{... | collective-permute-start | bytes 393224 | tf_op jit(solution)/shard_map/ppermute | solution.py:495
  37.6 17.3 %collective-permute-start.4 = (f32[128,256]{1,0:T(8,128)}, f32[128,256]{1,0:T(8,128)S(1)}, u32[]{:S(2)}, u32[]{:S(2)}) collective-permute-start(f32[128,256]{1,0:T(8,128)} %backward_light.1), channel_id=1, source_target_pairs={{16,0},{24,8},{17,1},{25,9},{18,2},{26,10},{19,3},{27,11},{20,4},{... | collective-permute-start | bytes 393224 | tf_op jit(solution)/shard_map/ppermute | solution.py:495
  79.3 11.2 %collective-permute-start.27 = (f32[704,128]{1,0:T(8,128)S(1)}, f32[704,128]{1,0:T(8,128)S(1)}, u32[]{:S(2)}, u32[]{:S(2)}) collective-permute-start(f32[704,128]{1,0:T(8,128)S(1)} %get-tuple-element.55), channel_id=1, source_target_pairs={{0,2},{1,3},{2,0},{3,1},{4,6},{5,7},{6,4},{7,5},{8,10},{9,11},{10,... | collective-permute-start | bytes 1081352 | tf_op jit(solution)/shard_map/ppermute | solution.py:490
  81.8 10.2 %collective-permute-start.17 = (f32[704,128]{1,0:T(8,128)S(1)}, f32[704,128]{1,0:T(8,128)S(1)}, u32[]{:S(2)}, u32[]{:S(2)}) collective-permute-start(f32[704,128]{1,0:T(8,128)S(1)} %get-tuple-element.56), channel_id=1, source_target_pairs={{0,1},{1,0},{2,3},{3,2},{4,5},{5,4},{6,7},{7,6},{8,9},{9,8},{10,11... | collective-permute-start | bytes 1081352 | tf_op jit(solution)/shard_map/ppermute | solution.py:490
  83.4 9.9 %collective-permute-start.7 = (f32[704,128]{1,0:T(8,128)S(1)}, f32[704,128]{1,0:T(8,128)S(1)}, u32[]{:S(2)}, u32[]{:S(2)}) collective-permute-start(f32[704,128]{1,0:T(8,128)S(1)} %get-tuple-element.57), channel_id=1, source_target_pairs={{0,16},{8,24},{16,0},{24,8},{1,17},{9,25},{17,1},{25,9},{2,18},{10... | collective-permute-start | bytes 1081352 | tf_op jit(solution)/shard_map/ppermute | solution.py:490
  93.4 5.6 %collective-permute-start.28 = (f32[352,128]{1,0:T(8,128)S(1)}, f32[352,128]{1,0:T(8,128)S(1)}, u32[]{:S(2)}, u32[]{:S(2)}) collective-permute-start(f32[352,128]{1,0:T(8,128)S(1)} %get-tuple-element.52), channel_id=1, source_target_pairs={{0,16},{8,24},{16,0},{24,8},{1,17},{9,25},{17,1},{25,9},{2,18},{10... | collective-permute-start | bytes 540680 | tf_op jit(solution)/shard_map/ppermute | solution.py:490
  93.8 5.5 %collective-permute-start.18 = (f32[352,128]{1,0:T(8,128)S(1)}, f32[352,128]{1,0:T(8,128)S(1)}, u32[]{:S(2)}, u32[]{:S(2)}) collective-permute-start(f32[352,128]{1,0:T(8,128)S(1)} %get-tuple-element.53), channel_id=1, source_target_pairs={{0,2},{1,3},{2,0},{3,1},{4,6},{5,7},{6,4},{7,5},{8,10},{9,11},{10,... | collective-permute-start | bytes 540680 | tf_op jit(solution)/shard_map/ppermute | solution.py:490
  94.2 5.5 %collective-permute-start.8 = (f32[352,128]{1,0:T(8,128)S(1)}, f32[352,128]{1,0:T(8,128)S(1)}, u32[]{:S(2)}, u32[]{:S(2)}) collective-permute-start(f32[352,128]{1,0:T(8,128)S(1)} %get-tuple-element.54), channel_id=1, source_target_pairs={{0,1},{1,0},{2,3},{3,2},{4,5},{5,4},{6,7},{7,6},{8,9},{9,8},{10,11... | collective-permute-start | bytes 540680 | tf_op jit(solution)/shard_map/ppermute | solution.py:490
  100.2 6.8 %collective-permute-start.19 = (f32[176,128]{1,0:T(8,128)S(1)}, f32[176,128]{1,0:T(8,128)S(1)}, u32[]{:S(2)}, u32[]{:S(2)}) collective-permute-start(f32[176,128]{1,0:T(8,128)S(1)} %get-tuple-element.50), channel_id=1, source_target_pairs={{0,16},{8,24},{16,0},{24,8},{1,17},{9,25},{17,1},{25,9},{2,18},{10... | collective-permute-start | bytes 270344 | tf_op jit(solution)/shard_map/ppermute | solution.py:490
  102.0 5.1 %collective-permute-start.9 = (f32[176,128]{1,0:T(8,128)S(1)}, f32[176,128]{1,0:T(8,128)S(1)}, u32[]{:S(2)}, u32[]{:S(2)}) collective-permute-start(f32[176,128]{1,0:T(8,128)S(1)} %get-tuple-element.51), channel_id=1, source_target_pairs={{0,2},{1,3},{2,0},{3,1},{4,6},{5,7},{6,4},{7,5},{8,10},{9,11},{10,... | collective-permute-start | bytes 270344 | tf_op jit(solution)/shard_map/ppermute | solution.py:490
  104.4 5.0 %collective-permute-start.30 = (f32[88,128]{1,0:T(8,128)S(1)}, f32[88,128]{1,0:T(8,128)S(1)}, u32[]{:S(2)}, u32[]{:S(2)}) collective-permute-start(f32[88,128]{1,0:T(8,128)S(1)} %slice_add_fusion.18), channel_id=1, source_target_pairs={{0,4},{1,5},{2,6},{3,7},{4,0},{5,1},{6,2},{7,3},{8,12},{9,13},{10,... | collective-permute-start | bytes 135176 | tf_op jit(solution)/shard_map/ppermute | solution.py:490
  109.5 6.6 %collective-permute-start.20 = (f32[88,128]{1,0:T(8,128)S(1)}, f32[88,128]{1,0:T(8,128)S(1)}, u32[]{:S(2)}, u32[]{:S(2)}) collective-permute-start(f32[88,128]{1,0:T(8,128)S(1)} %get-tuple-element.47), channel_id=1, source_target_pairs={{0,4},{1,5},{2,6},{3,7},{4,0},{5,1},{6,2},{7,3},{8,12},{9,13},{10,... | collective-permute-start | bytes 135176 | tf_op jit(solution)/shard_map/ppermute | solution.py:490
  112.6 5.3 %collective-permute-start.10 = (f32[88,128]{1,0:T(8,128)S(1)}, f32[88,128]{1,0:T(8,128)S(1)}, u32[]{:S(2)}, u32[]{:S(2)}) collective-permute-start(f32[88,128]{1,0:T(8,128)S(1)} %get-tuple-element.48), channel_id=1, source_target_pairs={{0,4},{1,5},{2,6},{3,7},{4,0},{5,1},{6,2},{7,3},{8,12},{9,13},{10,... | collective-permute-start | bytes 135176 | tf_op jit(solution)/shard_map/ppermute | solution.py:490
  112.7 25.3 %collective-permute-start.2 = (f32[8,128,256]{2,1,0:T(8,128)S(1)}, f32[8,128,256]{2,1,0:T(8,128)S(1)}, u32[]{:S(2)}, u32[]{:S(2)}) collective-permute-start(f32[8,128,256]{2,1,0:T(8,128)S(1)} %copy-done.24), channel_id=1, source_target_pairs={{0,8},{8,0},{16,24},{24,16},{1,9},{9,1},{17,25},{25,17},{2,10},{10... | collective-permute-start | bytes 3145736 | tf_op jit(solution)/shard_map/ppermute | solution.py:490
  112.7 26.0 %collective-permute-start.5 = (f32[8,128,256]{2,1,0:T(8,128)S(1)}, f32[8,128,256]{2,1,0:T(8,128)S(1)}, u32[]{:S(2)}, u32[]{:S(2)}) collective-permute-start(f32[8,128,256]{2,1,0:T(8,128)S(1)} %copy-done.25), channel_id=1, source_target_pairs={{0,8},{8,0},{16,24},{24,16},{1,9},{9,1},{17,25},{25,17},{2,10},{10... | collective-permute-start | bytes 3145736 | tf_op jit(solution)/shard_map/ppermute | solution.py:490
  113.2 7.8 %collective-permute-start.31 = (f32[88,128]{1,0:T(8,128)S(1)}, f32[88,128]{1,0:T(8,128)S(1)}, u32[]{:S(2)}, u32[]{:S(2)}) collective-permute-start(f32[88,128]{1,0:T(8,128)S(1)} %get-tuple-element.46), channel_id=1, source_target_pairs={{0,4},{1,5},{2,6},{3,7},{4,0},{5,1},{6,2},{7,3},{8,12},{9,13},{10,... | collective-permute-start | bytes 135176 | tf_op jit(solution)/shard_map/ppermute | solution.py:490
  118.0 5.0 %collective-permute-start.11 = (f32[88,128]{1,0:T(8,128)S(1)}, f32[88,128]{1,0:T(8,128)S(1)}, u32[]{:S(2)}, u32[]{:S(2)}) collective-permute-start(f32[88,128]{1,0:T(8,128)S(1)} %get-tuple-element.59), channel_id=1, source_target_pairs={{0,4},{1,5},{2,6},{3,7},{4,0},{5,1},{6,2},{7,3},{8,12},{9,13},{10,... | collective-permute-start | bytes 135176 | tf_op jit(solution)/shard_map/ppermute | solution.py:490
  118.1 7.3 %collective-permute-start.21 = (f32[88,128]{1,0:T(8,128)S(1)}, f32[88,128]{1,0:T(8,128)S(1)}, u32[]{:S(2)}, u32[]{:S(2)}) collective-permute-start(f32[88,128]{1,0:T(8,128)S(1)} %get-tuple-element.58), channel_id=1, source_target_pairs={{0,4},{1,5},{2,6},{3,7},{4,0},{5,1},{6,2},{7,3},{8,12},{9,13},{10,... | collective-permute-start | bytes 135176 | tf_op jit(solution)/shard_map/ppermute | solution.py:490
  121.0 6.5 %collective-permute-start.32 = (f32[176,128]{1,0:T(8,128)S(1)}, f32[176,128]{1,0:T(8,128)S(1)}, u32[]{:S(2)}, u32[]{:S(2)}) collective-permute-start(f32[176,128]{1,0:T(8,128)S(1)} %pad_maximum_fusion.8), channel_id=1, source_target_pairs={{0,1},{1,0},{2,3},{3,2},{4,5},{5,4},{6,7},{7,6},{8,9},{9,8},{10,11... | collective-permute-start | bytes 270344 | tf_op jit(solution)/shard_map/ppermute | solution.py:490
  123.0 5.1 %collective-permute-start.12 = (f32[176,128]{1,0:T(8,128)S(1)}, f32[176,128]{1,0:T(8,128)S(1)}, u32[]{:S(2)}, u32[]{:S(2)}) collective-permute-start(f32[176,128]{1,0:T(8,128)S(1)} %pad_maximum_fusion.6), channel_id=1, source_target_pairs={{0,2},{1,3},{2,0},{3,1},{4,6},{5,7},{6,4},{7,5},{8,10},{9,11},{10,... | collective-permute-start | bytes 270344 | tf_op jit(solution)/shard_map/ppermute | solution.py:490
  125.4 4.6 %collective-permute-start.22 = (f32[176,128]{1,0:T(8,128)S(1)}, f32[176,128]{1,0:T(8,128)S(1)}, u32[]{:S(2)}, u32[]{:S(2)}) collective-permute-start(f32[176,128]{1,0:T(8,128)S(1)} %pad_maximum_fusion.7), channel_id=1, source_target_pairs={{0,16},{8,24},{16,0},{24,8},{1,17},{9,25},{17,1},{25,9},{2,18},{10... | collective-permute-start | bytes 270344 | tf_op jit(solution)/shard_map/ppermute | solution.py:490
  127.4 5.6 %collective-permute-start.33 = (f32[352,128]{1,0:T(8,128)S(1)}, f32[352,128]{1,0:T(8,128)S(1)}, u32[]{:S(2)}, u32[]{:S(2)}) collective-permute-start(f32[352,128]{1,0:T(8,128)S(1)} %pad_maximum_fusion.5), channel_id=1, source_target_pairs={{0,16},{8,24},{16,0},{24,8},{1,17},{9,25},{17,1},{25,9},{2,18},{10... | collective-permute-start | bytes 540680 | tf_op jit(solution)/shard_map/ppermute | solution.py:490
  128.1 5.6 %collective-permute-start.13 = (f32[352,128]{1,0:T(8,128)S(1)}, f32[352,128]{1,0:T(8,128)S(1)}, u32[]{:S(2)}, u32[]{:S(2)}) collective-permute-start(f32[352,128]{1,0:T(8,128)S(1)} %pad_maximum_fusion.3), channel_id=1, source_target_pairs={{0,1},{1,0},{2,3},{3,2},{4,5},{5,4},{6,7},{7,6},{8,9},{9,8},{10,11... | collective-permute-start | bytes 540680 | tf_op jit(solution)/shard_map/ppermute | solution.py:490
  130.1 6.5 %collective-permute-start.23 = (f32[352,128]{1,0:T(8,128)S(1)}, f32[352,128]{1,0:T(8,128)S(1)}, u32[]{:S(2)}, u32[]{:S(2)}) collective-permute-start(f32[352,128]{1,0:T(8,128)S(1)} %pad_maximum_fusion.4), channel_id=1, source_target_pairs={{0,2},{1,3},{2,0},{3,1},{4,6},{5,7},{6,4},{7,5},{8,10},{9,11},{10,... | collective-permute-start | bytes 540680 | tf_op jit(solution)/shard_map/ppermute | solution.py:490
  133.0 7.5 %collective-permute-start.34 = (f32[704,128]{1,0:T(8,128)S(1)}, f32[704,128]{1,0:T(8,128)S(1)}, u32[]{:S(2)}, u32[]{:S(2)}) collective-permute-start(f32[704,128]{1,0:T(8,128)S(1)} %pad_maximum_fusion.2.rest_8_), channel_id=1, source_target_pairs={{0,2},{1,3},{2,0},{3,1},{4,6},{5,7},{6,4},{7,5},{8,10},{9,11},{10,... | collective-permute-start | bytes 1081352 | tf_op jit(solution)/shard_map/ppermute | solution.py:490
  133.6 6.9 %collective-permute-start.35 = (f32[704,128]{1,0:T(8,128)S(1)}, f32[704,128]{1,0:T(8,128)S(1)}, u32[]{:S(2)}, u32[]{:S(2)}) collective-permute-start(f32[704,128]{1,0:T(8,128)S(1)} %pad_maximum_fusion.2.rest_8_), channel_id=1, source_target_pairs={{0,8},{8,0},{16,24},{24,16},{1,9},{9,1},{17,25},{25,17},{2,10},{10... | collective-permute-start | bytes 1081352 | tf_op jit(solution)/shard_map/ppermute | solution.py:490
  136.5 8.6 %collective-permute-start.14 = (f32[704,128]{1,0:T(8,128)S(1)}, f32[704,128]{1,0:T(8,128)S(1)}, u32[]{:S(2)}, u32[]{:S(2)}) collective-permute-start(f32[704,128]{1,0:T(8,128)S(1)} %pad_maximum_fusion.rest_0_), channel_id=1, source_target_pairs={{0,16},{8,24},{16,0},{24,8},{1,17},{9,25},{17,1},{25,9},{2,18},{10... | collective-permute-start | bytes 1081352 | tf_op jit(solution)/shard_map/ppermute | solution.py:490
  138.0 8.7 %collective-permute-start.24 = (f32[704,128]{1,0:T(8,128)S(1)}, f32[704,128]{1,0:T(8,128)S(1)}, u32[]{:S(2)}, u32[]{:S(2)}) collective-permute-start(f32[704,128]{1,0:T(8,128)S(1)} %pad_maximum_fusion.1.rest_4_), channel_id=1, source_target_pairs={{0,1},{1,0},{2,3},{3,2},{4,5},{5,4},{6,7},{7,6},{8,9},{9,8},{10,11... | collective-permute-start | bytes 1081352 | tf_op jit(solution)/shard_map/ppermute | solution.py:490
  138.6 8.3 %collective-permute-start.15 = (f32[704,128]{1,0:T(8,128)S(1)}, f32[704,128]{1,0:T(8,128)S(1)}, u32[]{:S(2)}, u32[]{:S(2)}) collective-permute-start(f32[704,128]{1,0:T(8,128)S(1)} %pad_maximum_fusion.rest_0_), channel_id=1, source_target_pairs={{0,8},{8,0},{16,24},{24,16},{1,9},{9,1},{17,25},{25,17},{2,10},{10... | collective-permute-start | bytes 1081352 | tf_op jit(solution)/shard_map/ppermute | solution.py:490
  140.5 6.5 %collective-permute-start.25 = (f32[704,128]{1,0:T(8,128)S(1)}, f32[704,128]{1,0:T(8,128)S(1)}, u32[]{:S(2)}, u32[]{:S(2)}) collective-permute-start(f32[704,128]{1,0:T(8,128)S(1)} %pad_maximum_fusion.1.rest_4_), channel_id=1, source_target_pairs={{0,8},{8,0},{16,24},{24,16},{1,9},{9,1},{17,25},{25,17},{2,10},{10... | collective-permute-start | bytes 1081352 | tf_op jit(solution)/shard_map/ppermute | solution.py:490
  140.6 6.5 %collective-permute-start.36 = (f32[704,128]{1,0:T(8,128)S(1)}, f32[704,128]{1,0:T(8,128)S(1)}, u32[]{:S(2)}, u32[]{:S(2)}) collective-permute-start(f32[704,128]{1,0:T(8,128)S(1)} %collective-permute-done.34.rest_9_), channel_id=1, source_target_pairs={{0,8},{8,0},{16,24},{24,16},{1,9},{9,1},{17,25},{25,17},{2,10},{10... | collective-permute-start | bytes 1081352 | tf_op jit(solution)/shard_map/ppermute | solution.py:490
  (31 other events, 254.5 us)
